TPU v7x, 32 devices: a whole 2x2x4 slice. The times are simulated.
32 devices in a mesh: ctx: 8 (over z, core), grp: 4 (over y, x).
Axes of the slice: x: 2, y: 2, z: 4, core: 2. Of those that a mesh axis runs over, the one named last changes fastest.
Arguments:
- queries: bfloat16 [2048, 8192], P('ctx', 'grp'), may hold values from -27 to 27, as said below
- keys: bfloat16 [2048, 1024], P('ctx'), may hold values from -27 to 27
- values: bfloat16 [2048, 1024], P('ctx'), may hold values from -6 to 6
- out_weight: bfloat16 [8192, 8192], P('grp'), may hold values from -0.0625 to 0.0625
- span_order: int32 [16], replicated, may hold values from 0 to 15, each once
- document: int32 [2048], replicated, may hold values from 0 to 3, never falling along the last dimension, each value on 1 to 1024 neighbouring positions
Outputs:
- projected: bfloat16 [2048, 8192], P('ctx', 'grp')
Inputs may be any that keep to these rules, and one draw needn't show every extreme that they name: `queries`: queries and keys are of order one, except a few rows that may be larger.
All inputs are finite; a program needn't handle non-finite values.
Results may differ from a plain program's by a relative error of at most 0.023.
Values may be sent and summed in bfloat16 or wider, within the bound.
A program may use at most 128 MiB of HBM per device.

v0:
```python
import functools
import math

import jax
import jax.numpy as jnp
from jax import lax
from jax.experimental import pallas as pl
from jax.experimental.pallas import tpu as pltpu
from jax.sharding import PartitionSpec as P

HEAD_DIM = 128
QUERY_GROUP = 8
CORES = 2
MESH = pl.DeviceIdType.MESH
HIDDEN = -1e30
UNROLL = 4


def gather_attend_kernel(
    n_ctx, kv_heads, first_of, order_ref, doc_rows, q_ref, k_hbm, v_hbm, out_ref,
    k_all, v_all, row_doc_ref, bias_ref, max_ref, acc_ref, local_sem, send_sem, recv_sem,
):
    nz = n_ctx // CORES
    me = lax.axis_index("ctx")
    group = lax.axis_index("grp")
    z, core = me // CORES, me % CORES
    partner = z * CORES + 1 - core
    tok_rows, width = k_all.shape[1], k_all.shape[2]
    span = tok_rows // 2
    heads = q_ref.shape[1] // HEAD_DIM
    shared = heads // kv_heads
    start = pl.multiple_of(first_of(group) * HEAD_DIM, HEAD_DIM)
    alls = (k_all, v_all)
    loads = [
        pltpu.make_async_copy(src.at[:, pl.ds(start, width)], dst.at[me], local_sem.at[i])
        for i, (src, dst) in enumerate(((k_hbm, k_all), (v_hbm, v_all)))
    ]
    for load in loads:
        load.start()
    barrier = pltpu.get_barrier_semaphore()
    pl.semaphore_signal(barrier, inc=1, device_id=(partner, group), device_id_type=MESH)

    @pl.when(z > 0)
    def _():
        pl.semaphore_signal(barrier, inc=1, device_id=(me - CORES, group), device_id_type=MESH)

    @pl.when(z < nz - 1)
    def _():
        pl.semaphore_signal(barrier, inc=1, device_id=(me + CORES, group), device_id_type=MESH)

    pl.semaphore_wait(barrier, 1 + jnp.minimum(z, 1) + jnp.minimum(nz - 1 - z, 1))

    def piece(way, part, chip, target):
        block = chip * CORES + core
        return pltpu.make_async_remote_copy(
            src_ref=alls[part].at[block],
            dst_ref=alls[part].at[block],
            send_sem=send_sem.at[way, part, chip],
            recv_sem=recv_sem.at[part, block],
            device_id=(target, group),
            device_id_type=MESH,
        )

    for part in range(2):
        loads[part].wait()

        @pl.when(z < nz - 1)
        def _():
            piece(0, part, z, me + CORES).start()

        @pl.when(z > 0)
        def _():
            piece(1, part, z, me - CORES).start()

        piece(2, part, z, partner).start()

    def arrived(part, chip, from_core):
        block = chip * CORES + from_core
        pltpu.make_async_copy(
            alls[part].at[block], alls[part].at[block], recv_sem.at[part, block]
        ).wait()

    max_ref[...] = jnp.full(max_ref.shape, HIDDEN, jnp.float32)
    acc_ref[...] = jnp.zeros(acc_ref.shape, jnp.float32)
    for r in range(2):
        row_doc_ref[r] = jnp.transpose(
            jnp.broadcast_to(doc_rows[order_ref[me * 2 + r]], (span, span))
        )

    factor = math.log2(math.e) / math.sqrt(HEAD_DIM)
    keys_per_step = CORES * tok_rows
    parts_of_keys = keys_per_step // HEAD_DIM
    row_at = lax.broadcasted_iota(jnp.int32, (span, span), 0)
    col_at = lax.broadcasted_iota(jnp.int32, (span, span), 1)
    near = jnp.minimum(z, nz - 1 - z)
    long_way = jnp.where(z < nz - 1 - z, 1, -1)

    def step(n, carry):
        for part in range(2):

            @pl.when((n > 0) & (z - n >= 0))
            def _():
                arrived(part, z - n, core)

                @pl.when(z < nz - 1)
                def _():
                    piece(0, part, z - n, me + CORES).start()

                piece(2, part, z - n, partner).start()

            @pl.when((n > 0) & (z + n < nz))
            def _():
                arrived(part, z + n, core)

                @pl.when(z > 0)
                def _():
                    piece(1, part, z + n, me - CORES).start()

                piece(2, part, z + n, partner).start()

        away = (n + 1) // 2
        paired = z + away * (1 - 2 * (n % 2))
        chip = jnp.where(n <= 2 * near, paired, z + long_way * (n - near))

        for slot in range(2 * CORES):
            key_span = order_ref[chip * (2 * CORES) + slot]
            key_doc = doc_rows[key_span]
            for r in range(2):
                mine = order_ref[me * 2 + r]
                seen = (key_doc == row_doc_ref[r]) & (
                    key_span * span + col_at <= mine * span + row_at
                )
                bias_ref[r * span : (r + 1) * span, slot * span : (slot + 1) * span] = jnp.where(
                    seen, 0.0, HIDDEN
                )

        for part in range(2):
            arrived(part, chip, 1 - core)

        for h in range(kv_heads):
            cols = slice(h * HEAD_DIM, (h + 1) * HEAD_DIM)

            def some_heads(at, carry):
                key = k_all[pl.ds(chip * CORES, CORES), :, cols].reshape(keys_per_step, HEAD_DIM)
                value = v_all[pl.ds(chip * CORES, CORES), :, cols].reshape(
                    keys_per_step, HEAD_DIM
                )
                value = jnp.concatenate([value, jnp.ones_like(value)], axis=1)
                picked = [h * shared + at * UNROLL + u for u in range(UNROLL)]
                scores = [
                    lax.dot_general(
                        q_ref[:, pl.ds(pl.multiple_of(head * HEAD_DIM, HEAD_DIM), HEAD_DIM)],
                        key,
                        (((1,), (1,)), ((), ())),
                        preferred_element_type=jnp.float32,
                    )
                    + bias_ref[...]
                    for head in picked
                ]
                olds = [max_ref[head] for head in picked]
                sums = [acc_ref[head] for head in picked]
                results = []
                for score, old, total in zip(scores, olds, sums):
                    top = jnp.maximum(old, jnp.max(score, axis=1, keepdims=True))
                    rescale = jnp.exp2((old - top) * factor)
                    probs = jnp.concatenate(
                        [
                            jnp.exp2(
                                (score[:, c * HEAD_DIM : (c + 1) * HEAD_DIM] - top) * factor
                            ).astype(jnp.bfloat16)
                            for c in range(parts_of_keys)
                        ],
                        axis=1,
                    )
                    mixed = jnp.dot(probs, value, preferred_element_type=jnp.float32)
                    both = jnp.concatenate([rescale, rescale], axis=1)
                    results.append((top, total * both + mixed))
                for head, (top, total) in zip(picked, results):
                    max_ref[head] = top
                    acc_ref[head] = total
                return carry

            lax.fori_loop(0, shared // UNROLL, some_heads, 0)
        return carry

    lax.fori_loop(0, nz, step, 0)

    for head in range(heads):
        total = acc_ref[head]
        out_ref[:, head * HEAD_DIM : (head + 1) * HEAD_DIM] = (
            total[:, :HEAD_DIM] / total[:, HEAD_DIM:]
        ).astype(out_ref.dtype)

    for part in range(2):
        for chip in range(nz):
            piece(2, part, chip, partner).wait_send()

            @pl.when((z < nz - 1) & (chip <= z))
            def _():
                piece(0, part, chip, me + CORES).wait_send()

            @pl.when((z > 0) & (chip >= z))
            def _():
                piece(1, part, chip, me - CORES).wait_send()


def gather_attend(queries, keys, values, span_order, document, n_ctx, kv_heads, first_of):
    slots = span_order.shape[0]
    span = document.shape[0] // slots
    rows = queries.shape[0]
    heads = queries.shape[1] // HEAD_DIM
    smem = pl.BlockSpec(memory_space=pltpu.SMEM)
    vmem = pl.BlockSpec(memory_space=pltpu.VMEM)
    hbm = pl.BlockSpec(memory_space=pl.ANY)
    f32, bf16 = jnp.float32, jnp.bfloat16
    return pl.pallas_call(
        functools.partial(gather_attend_kernel, n_ctx, kv_heads, first_of),
        out_shape=jax.ShapeDtypeStruct(queries.shape, queries.dtype),
        in_specs=[smem, vmem, vmem, hbm, hbm],
        out_specs=vmem,
        scratch_shapes=[
            pltpu.VMEM((n_ctx, rows, kv_heads * HEAD_DIM), bf16),
            pltpu.VMEM((n_ctx, rows, kv_heads * HEAD_DIM), bf16),
            pltpu.VMEM((2, span, span), jnp.int32),
            pltpu.VMEM((rows, CORES * rows), f32),
            pltpu.VMEM((heads, rows, HEAD_DIM), f32),
            pltpu.VMEM((heads, rows, 2 * HEAD_DIM), f32),
            pltpu.SemaphoreType.DMA((2,)),
            pltpu.SemaphoreType.DMA((3, 2, n_ctx // CORES)),
            pltpu.SemaphoreType.DMA((2, n_ctx)),
        ],
        compiler_params=pltpu.CompilerParams(collective_id=0, has_side_effects=True),
        name="gather_attend",
    )(span_order, document.reshape(slots, 1, span), queries, keys, values)


def project_kernel(
    att_ref, w_hbm, out_ref, w_buf, send_one, got_one, send_two, got_two, own_ref,
    w_sem, sent_one, recv_one, sent_two, recv_two,
):
    me = lax.axis_index("ctx")
    group = lax.axis_index("grp")
    side = group + 1 - 2 * (group % 2)
    other = (group + 2) % 4
    far = 3 - group
    steps, _, width = w_buf.shape
    block_width = out_ref.shape[1]

    def path_sub(i):
        path = i % 2
        return path, 2 * path + (i // 2) % 2

    def block_of(i):
        path = i % 2
        first = far if i < 4 else (other if path else side)
        return first if i < 8 else ((side if path else other) if i < 12 else group)

    def fetch(i, block, sub):
        start = pl.multiple_of(block * block_width + sub * width, width)
        return pltpu.make_async_copy(w_hbm.at[:, pl.ds(start, width)], w_buf.at[i], w_sem.at[i])

    for i in range(steps):
        fetch(i, block_of(i), path_sub(i)[1]).start()

    barrier = pltpu.get_barrier_semaphore()
    for target in (side, other):
        pl.semaphore_signal(barrier, inc=1, device_id=(me, target), device_id_type=MESH)
    pl.semaphore_wait(barrier, 2)

    def product(i):
        fetch(i, group, 0).wait()
        return jnp.dot(att_ref[...], w_buf[i], preferred_element_type=jnp.float32)

    def stage_one(i):
        path = i % 2
        return pltpu.make_async_remote_copy(
            src_ref=send_one.at[i],
            dst_ref=got_one.at[i],
            send_sem=sent_one.at[i],
            recv_sem=recv_one.at[i],
            device_id=(me, (1 - path) * side + path * other),
            device_id_type=MESH,
        )

    def stage_two(j):
        path = j % 2
        return pltpu.make_async_remote_copy(
            src_ref=send_two.at[j],
            dst_ref=got_two.at[j],
            send_sem=sent_two.at[j],
            recv_sem=recv_two.at[j],
            device_id=(me, (1 - path) * other + path * side),
            device_id_type=MESH,
        )

    def first(i, carry):
        send_one[i] = product(i).astype(send_one.dtype)
        stage_one(i).start()
        return carry

    lax.fori_loop(0, 8, first, 0)

    def second(j, carry):
        part = product(8 + j)
        stage_one(j).wait_recv()
        send_two[j] = (part + got_one[j].astype(jnp.float32)).astype(send_two.dtype)
        stage_two(j).start()
        return carry

    lax.fori_loop(0, 4, second, 0)

    def third(j, carry):
        own_ref[j] = product(12 + j)
        return carry

    lax.fori_loop(0, 4, third, 0)

    for j in range(4):
        stage_one(4 + j).wait_recv()
        own_ref[j] = own_ref[j] + got_one[4 + j].astype(jnp.float32)
    for j in range(4):
        stage_two(j).wait_recv()
        at = path_sub(j)[1] * width
        out_ref[:, at : at + width] = (own_ref[j] + got_two[j].astype(jnp.float32)).astype(
            out_ref.dtype
        )
    for i in range(8):
        stage_one(i).wait_send()
    for j in range(4):
        stage_two(j).wait_send()


def project(attended, out_weight):
    rows, depth = attended.shape
    features = out_weight.shape[1]
    width = features // 16
    bf16, f32 = jnp.bfloat16, jnp.float32
    return pl.pallas_call(
        project_kernel,
        out_shape=jax.ShapeDtypeStruct((rows, features // 4), bf16),
        in_specs=[pl.BlockSpec(memory_space=pltpu.VMEM), pl.BlockSpec(memory_space=pl.ANY)],
        out_specs=pl.BlockSpec(memory_space=pltpu.VMEM),
        scratch_shapes=[
            pltpu.VMEM((16, depth, width), bf16),
            pltpu.VMEM((8, rows, width), bf16),
            pltpu.VMEM((8, rows, width), bf16),
            pltpu.VMEM((4, rows, width), bf16),
            pltpu.VMEM((4, rows, width), bf16),
            pltpu.VMEM((4, rows, width), f32),
            pltpu.SemaphoreType.DMA((16,)),
            pltpu.SemaphoreType.DMA((8,)),
            pltpu.SemaphoreType.DMA((8,)),
            pltpu.SemaphoreType.DMA((4,)),
            pltpu.SemaphoreType.DMA((4,)),
        ],
        compiler_params=pltpu.CompilerParams(
            collective_id=1, has_side_effects=True, vmem_limit_bytes=60 * 1024 * 1024
        ),
        name="project",
    )(attended, out_weight)


def shards(n_ctx, n_grp, queries, keys, values, out_weight, span_order, document):
    local_heads = queries.shape[1] // HEAD_DIM
    kv_heads = max(1, local_heads // QUERY_GROUP)
    attended = gather_attend(
        queries, keys, values, span_order, document, n_ctx, kv_heads,
        lambda group: group * local_heads // QUERY_GROUP,
    )
    if n_grp == 4:
        return project(attended, out_weight)
    partial_value = jnp.dot(attended, out_weight, preferred_element_type=jnp.float32)
    return lax.psum_scatter(
        partial_value.astype(jnp.bfloat16), "grp", scatter_dimension=1, tiled=True
    )


def solution(mesh):
    in_specs = (P("ctx", "grp"), P("ctx", None), P("ctx", None), P("grp", None), P(), P())
    body = functools.partial(shards, mesh.shape["ctx"], mesh.shape["grp"])
    return jax.shard_map(
        body, mesh=mesh, in_specs=in_specs, out_specs=P("ctx", "grp"), check_vma=False
    )
```

profile of v0, /device:TPU:0, one launch (start us, length us, event | category | flops | bytes accessed | tf_op | source)
XLA Modules:
  0.0 74.5 jit_solution(3128795720409736301)
XLA Ops:
  0.0 29.9 %gather_attend.1.att_ref = bf16[256,2048]{1,0:T(8,128)(2,1)} custom-call(s32[16]{0:T(128)} %order_ref.1, s32[16,1,128]{2,1,0:T(1,128)} %bitcast.1, bf16[256,2048]{1,0:T(8,128)(2,1)} %q_ref.1, bf16[256,1024]{1,0:T(8,128)(2,1)} %k_hbm.1, bf16[256,1024]{1,0:T(8,128)(2,1)} %v_hbm.1), custom_call_target="tpu_custom_call" | custom-call | tf_op jit(solution)/shard_map/gather_attend/pallas_call | solution.py:216
  29.9 42.2 %project.1 = bf16[256,2048]{1,0:T(8,128)(2,1)} custom-call(bf16[256,2048]{1,0:T(8,128)(2,1)} %gather_attend.1.att_ref, bf16[2048,8192]{1,0:T(8,128)(2,1)} %w_hbm.1), custom_call_target="tpu_custom_call" | custom-call | tf_op jit(solution)/shard_map/project/pallas_call | solution.py:338
  72.1 2.3 %copy.8 = bf16[256,2048]{1,0:T(8,128)(2,1)} copy(bf16[256,2048]{1,0:T(8,128)(2,1)} %project.1) | data formatting | bytes 2097152
where the time goes:
time: 74.7 us; the launch traced here: 74.5 us
  Pallas kernels  72.1 us (97%)
  local copies, waits for them, and re-layouts  2.3 us (3%)
    pallas_call x1, Pallas kernels, project(): pl.pallas_call(project_kernel, out_shape=jax.ShapeDtypeStruct((rows, feat...  42.2 us
    pallas_call x1, Pallas kernels, gather_attend(): pl.pallas_call(functools.partial(gather_attend_kernel, n_ctx, kv_heads, f...  29.9 us
    unnamed x1, local copies, waits for them, and re-layouts  2.3 us

commit v1 on v0

v1 whole, which is shorter than its diff:
```python
import functools
import math
from types import SimpleNamespace

import jax
import jax.numpy as jnp
from jax import lax
from jax.experimental import pallas as pl
from jax.experimental.pallas import tpu as pltpu
from jax.sharding import PartitionSpec as P

HEAD_DIM = 128
QUERY_GROUP = 8
CORES = 2
MESH = pl.DeviceIdType.MESH
HIDDEN = -1e30
UNROLL = 4


def attention(
    n_ctx, kv_heads, first_of, greeted, order_ref, doc_rows, q_hbm, k_hbm, v_hbm,
    q_ref, kv_all, row_doc_ref, bias_ref, max_ref, acc_ref, local_sem, send_sem, recv_sem,
):
    nz = n_ctx // CORES
    me = lax.axis_index("ctx")
    group = lax.axis_index("grp")
    z, core = me // CORES, me % CORES
    partner = z * CORES + 1 - core
    tok_rows = kv_all.shape[2]
    span = doc_rows.shape[2]
    spans = tok_rows // span
    shared = q_ref.shape[1] // HEAD_DIM // kv_heads
    unroll = min(UNROLL, shared)
    factor = math.log2(math.e) / math.sqrt(HEAD_DIM)
    keys_per_step = CORES * tok_rows
    parts_of_keys = keys_per_step // HEAD_DIM
    near = jnp.minimum(z, nz - 1 - z)
    long_way = jnp.where(z < nz - 1 - z, 1, -1)

    def piece(way, h, chip, target):
        block = chip * CORES + core
        return pltpu.make_async_remote_copy(
            src_ref=kv_all.at[block, h],
            dst_ref=kv_all.at[block, h],
            send_sem=send_sem.at[way, h, chip],
            recv_sem=recv_sem.at[h, block],
            device_id=(target, group),
            device_id_type=MESH,
        )

    def arrived(h, chip, from_core):
        block = chip * CORES + from_core
        pltpu.make_async_copy(
            kv_all.at[block, h], kv_all.at[block, h], recv_sem.at[h, block]
        ).wait()

    def load(h, side):
        start = pl.multiple_of((first_of(group) + h) * HEAD_DIM, HEAD_DIM)
        return pltpu.make_async_copy(
            (k_hbm, v_hbm)[side].at[:, pl.ds(start, HEAD_DIM)],
            kv_all.at[me, h, :, pl.ds(side * HEAD_DIM, HEAD_DIM)],
            local_sem.at[h, side],
        )

    q_load = pltpu.make_async_copy(q_hbm, q_ref, local_sem.at[kv_heads, 0])

    def start():
        for h in range(kv_heads):
            for side in range(2):
                load(h, side).start()
        q_load.start()
        barrier = pltpu.get_barrier_semaphore()
        for target in [(partner, group)] + greeted:
            pl.semaphore_signal(barrier, inc=1, device_id=target, device_id_type=MESH)

        @pl.when(z > 0)
        def _():
            pl.semaphore_signal(
                barrier, inc=1, device_id=(me - CORES, group), device_id_type=MESH
            )

        @pl.when(z < nz - 1)
        def _():
            pl.semaphore_signal(
                barrier, inc=1, device_id=(me + CORES, group), device_id_type=MESH
            )

        pl.semaphore_wait(
            barrier, 1 + len(greeted) + jnp.minimum(z, 1) + jnp.minimum(nz - 1 - z, 1)
        )
        for h in range(kv_heads):
            for side in range(2):
                load(h, side).wait()

            @pl.when(z < nz - 1)
            def _():
                piece(0, h, z, me + CORES).start()

            @pl.when(z > 0)
            def _():
                piece(1, h, z, me - CORES).start()

            piece(2, h, z, partner).start()

    def prepare():
        max_ref[...] = jnp.full(max_ref.shape, HIDDEN, jnp.float32)
        acc_ref[...] = jnp.zeros(acc_ref.shape, jnp.float32)
        for r in range(spans):
            row_doc_ref[r] = jnp.transpose(
                jnp.broadcast_to(doc_rows[order_ref[me * spans + r]], (span, span))
            )
        q_load.wait()

    def pass_on(n, h):
        @pl.when((n > 0) & (z - n >= 0))
        def _():
            arrived(h, z - n, core)

            @pl.when(z < nz - 1)
            def _():
                piece(0, h, z - n, me + CORES).start()

            piece(2, h, z - n, partner).start()

        @pl.when((n > 0) & (z + n < nz))
        def _():
            arrived(h, z + n, core)

            @pl.when(z > 0)
            def _():
                piece(1, h, z + n, me - CORES).start()

            piece(2, h, z + n, partner).start()

    def chip_of(n):
        away = (n + 1) // 2
        paired = z + away * (1 - 2 * (n % 2))
        return jnp.where(n <= 2 * near, paired, z + long_way * (n - near))

    def look(chip):
        row_at = lax.broadcasted_iota(jnp.int32, (span, span), 0)
        col_at = lax.broadcasted_iota(jnp.int32, (span, span), 1)
        for slot in range(spans * CORES):
            key_span = order_ref[chip * (spans * CORES) + slot]
            key_doc = doc_rows[key_span]
            for r in range(spans):
                mine = order_ref[me * spans + r]
                seen = (key_doc == row_doc_ref[r]) & (
                    key_span * span + col_at <= mine * span + row_at
                )
                bias_ref[r * span : (r + 1) * span, slot * span : (slot + 1) * span] = jnp.where(
                    seen, 0.0, HIDDEN
                )

    def attend(chip, h, low, count):
        def some_heads(at, carry):
            both = kv_all[pl.ds(chip * CORES, CORES), h].reshape(keys_per_step, 2 * HEAD_DIM)
            key = both[:, :HEAD_DIM]
            value = both[:, HEAD_DIM:]
            value = jnp.concatenate([value, jnp.ones_like(value)], axis=1)
            picked = [h * shared + at * unroll + u for u in range(unroll)]
            rows = pl.ds(low, count)
            asked = jnp.concatenate(
                [
                    q_ref[rows, pl.ds(pl.multiple_of(head * HEAD_DIM, HEAD_DIM), HEAD_DIM)]
                    for head in picked
                ],
                axis=0,
            )
            scores = lax.dot_general(
                asked, key, (((1,), (1,)), ((), ())), preferred_element_type=jnp.float32
            )
            bias = bias_ref[rows, :]
            tops, rescales, probs = [], [], []
            for u, head in enumerate(picked):
                score = scores[u * count : (u + 1) * count] + bias
                old = max_ref[head, rows]
                top = jnp.maximum(old, jnp.max(score, axis=1, keepdims=True))
                tops.append(top)
                rescales.append(jnp.exp2((old - top) * factor))
                probs.append(
                    jnp.concatenate(
                        [
                            jnp.exp2(
                                (score[:, c * HEAD_DIM : (c + 1) * HEAD_DIM] - top) * factor
                            ).astype(jnp.bfloat16)
                            for c in range(parts_of_keys)
                        ],
                        axis=1,
                    )
                )
            mixed = jnp.dot(
                jnp.concatenate(probs, axis=0), value, preferred_element_type=jnp.float32
            )
            for u, head in enumerate(picked):
                max_ref[head, rows] = tops[u]
                scale = jnp.concatenate([rescales[u], rescales[u]], axis=1)
                acc_ref[head, rows] = (
                    acc_ref[head, rows] * scale + mixed[u * count : (u + 1) * count]
                )
            return carry

        lax.fori_loop(0, shared // unroll, some_heads, 0)

    def step(n, carry):
        chip = chip_of(n)
        look(chip)
        for h in range(kv_heads):
            pass_on(n, h)
            arrived(h, chip, 1 - core)
            attend(chip, h, 0, tok_rows)
        return carry

    def result(head, low, count):
        total = acc_ref[head, pl.ds(low, count)]
        return (total[:, :HEAD_DIM] / total[:, HEAD_DIM:]).astype(jnp.bfloat16)

    def drain():
        for h in range(kv_heads):
            for chip in range(nz):
                piece(2, h, chip, partner).wait_send()

                @pl.when((z < nz - 1) & (chip <= z))
                def _():
                    piece(0, h, chip, me + CORES).wait_send()

                @pl.when((z > 0) & (chip >= z))
                def _():
                    piece(1, h, chip, me - CORES).wait_send()

    return SimpleNamespace(**locals())


def attention_scratch(n_ctx, rows, heads, kv_heads, span):
    f32, bf16 = jnp.float32, jnp.bfloat16
    return [
        pltpu.VMEM((rows, heads * HEAD_DIM), bf16),
        pltpu.VMEM((n_ctx, kv_heads, rows, 2 * HEAD_DIM), bf16),
        pltpu.VMEM((rows // span, span, span), jnp.int32),
        pltpu.VMEM((rows, CORES * rows), f32),
        pltpu.VMEM((heads, rows, HEAD_DIM), f32),
        pltpu.VMEM((heads, rows, 2 * HEAD_DIM), f32),
        pltpu.SemaphoreType.DMA((kv_heads + 1, 2)),
        pltpu.SemaphoreType.DMA((3, kv_heads, n_ctx // CORES)),
        pltpu.SemaphoreType.DMA((kv_heads, n_ctx)),
    ]


def gather_attend_kernel(
    n_ctx, kv_heads, first_of, order_ref, doc_rows, q_hbm, k_hbm, v_hbm, out_ref, *scratch
):
    part = attention(
        n_ctx, kv_heads, first_of, [], order_ref, doc_rows, q_hbm, k_hbm, v_hbm, *scratch
    )
    part.start()
    part.prepare()
    lax.fori_loop(0, part.nz, part.step, 0)
    rows, width = out_ref.shape
    for head in range(width // HEAD_DIM):
        out_ref[:, head * HEAD_DIM : (head + 1) * HEAD_DIM] = part.result(head, 0, rows)
    part.drain()


def fused_kernel(
    n_ctx, kv_heads, first_of, order_ref, doc_rows, q_hbm, k_hbm, v_hbm, w_hbm, out_ref,
    att_ref, w_buf, send_one, got_one, send_two, got_two, own_ref,
    w_sem, sent_one, recv_one, sent_two, recv_two, *scratch,
):
    me = lax.axis_index("ctx")
    group = lax.axis_index("grp")
    side = group + 1 - 2 * (group % 2)
    other = (group + 2) % 4
    far = 3 - group
    pieces, _, width = w_buf.shape
    block_width = out_ref.shape[1]
    part = attention(
        n_ctx, kv_heads, first_of, [(me, side), (me, other)],
        order_ref, doc_rows, q_hbm, k_hbm, v_hbm, *scratch,
    )
    span, spans = part.span, part.spans
    heads = part.q_ref.shape[1] // HEAD_DIM

    def path_sub(i):
        path = i % 2
        return path, 2 * path + (i // 2) % 2

    def block_of(i):
        path = i % 2
        first = far if i < 4 else (other if path else side)
        return first if i < 8 else ((side if path else other) if i < 12 else group)

    def fetch(i, block, sub):
        start = pl.multiple_of(block * block_width + sub * width, width)
        return pltpu.make_async_copy(w_hbm.at[:, pl.ds(start, width)], w_buf.at[i], w_sem.at[i])

    def product(r, i):
        if r == 0:
            fetch(i, group, 0).wait()
        return jnp.dot(att_ref[r], w_buf[i], preferred_element_type=jnp.float32)

    def stage_one(r, i):
        path = i % 2
        return pltpu.make_async_remote_copy(
            src_ref=send_one.at[r, i],
            dst_ref=got_one.at[r, i],
            send_sem=sent_one.at[r, i],
            recv_sem=recv_one.at[r, i],
            device_id=(me, (1 - path) * side + path * other),
            device_id_type=MESH,
        )

    def stage_two(r, j):
        path = j % 2
        return pltpu.make_async_remote_copy(
            src_ref=send_two.at[r, j],
            dst_ref=got_two.at[r, j],
            send_sem=sent_two.at[r, j],
            recv_sem=recv_two.at[r, j],
            device_id=(me, (1 - path) * other + path * side),
            device_id_type=MESH,
        )

    def first(r, low, high):
        def one(i, carry):
            send_one[r, i] = product(r, i).astype(send_one.dtype)
            stage_one(r, i).start()
            return carry

        lax.fori_loop(low, high, one, 0)

    def second(r):
        def one(j, carry):
            value = product(r, 8 + j)
            stage_one(r, j).wait_recv()
            send_two[r, j] = (value + got_one[r, j].astype(jnp.float32)).astype(send_two.dtype)
            stage_two(r, j).start()
            return carry

        lax.fori_loop(0, 4, one, 0)

    def third(r):
        def one(j, carry):
            own_ref[r, j] = product(r, 12 + j)
            return carry

        lax.fori_loop(0, 4, one, 0)

    def add_first(r):
        for j in range(4):
            stage_one(r, 4 + j).wait_recv()
            own_ref[r, j] = own_ref[r, j] + got_one[r, 4 + j].astype(jnp.float32)

    def last(r):
        for j in range(4):
            stage_two(r, j).wait_recv()
            at = path_sub(j)[1] * width
            out_ref[r * span : (r + 1) * span, at : at + width] = (
                own_ref[r, j] + got_two[r, j].astype(jnp.float32)
            ).astype(out_ref.dtype)

    def normalise(r):
        for head in range(heads):
            att_ref[r, :, head * HEAD_DIM : (head + 1) * HEAD_DIM] = part.result(
                head, r * span, span
            )

    part.start()
    for i in range(pieces):
        fetch(i, block_of(i), path_sub(i)[1]).start()
    part.prepare()
    lax.fori_loop(0, part.nz - 1, part.step, 0)

    n = part.nz - 1
    chip = part.chip_of(n)
    part.look(chip)
    for h in range(kv_heads - 1):
        part.pass_on(n, h)
        part.arrived(h, chip, 1 - part.core)
        part.attend(chip, h, 0, spans * span)
    part.pass_on(n, kv_heads - 1)
    part.arrived(kv_heads - 1, chip, 1 - part.core)
    part.attend(chip, kv_heads - 1, 0, span)
    normalise(0)
    first(0, 0, 8)
    part.attend(chip, kv_heads - 1, span, span)
    normalise(1)
    first(1, 0, 4)
    second(0)
    first(1, 4, 8)
    third(0)
    second(1)
    third(1)
    add_first(0)
    last(0)
    add_first(1)
    last(1)
    for r in range(spans):
        for i in range(8):
            stage_one(r, i).wait_send()
        for j in range(4):
            stage_two(r, j).wait_send()
    part.drain()


def fused(queries, keys, values, out_weight, span_order, document, n_ctx, kv_heads, first_of):
    slots = span_order.shape[0]
    span = document.shape[0] // slots
    rows, depth = queries.shape
    features = out_weight.shape[1]
    width = features // 16
    spans = rows // span
    f32, bf16 = jnp.float32, jnp.bfloat16
    hbm = pl.BlockSpec(memory_space=pl.ANY)
    vmem = pl.BlockSpec(memory_space=pltpu.VMEM)
    return pl.pallas_call(
        functools.partial(fused_kernel, n_ctx, kv_heads, first_of),
        out_shape=jax.ShapeDtypeStruct((rows, features // 4), bf16),
        in_specs=[pl.BlockSpec(memory_space=pltpu.SMEM), vmem, hbm, hbm, hbm, hbm],
        out_specs=vmem,
        scratch_shapes=[
            pltpu.VMEM((spans, span, depth), bf16),
            pltpu.VMEM((16, depth, width), bf16),
            pltpu.VMEM((spans, 8, span, width), bf16),
            pltpu.VMEM((spans, 8, span, width), bf16),
            pltpu.VMEM((spans, 4, span, width), bf16),
            pltpu.VMEM((spans, 4, span, width), bf16),
            pltpu.VMEM((spans, 4, span, width), f32),
            pltpu.SemaphoreType.DMA((16,)),
            pltpu.SemaphoreType.DMA((spans, 8)),
            pltpu.SemaphoreType.DMA((spans, 8)),
            pltpu.SemaphoreType.DMA((spans, 4)),
            pltpu.SemaphoreType.DMA((spans, 4)),
        ]
        + attention_scratch(n_ctx, rows, depth // HEAD_DIM, kv_heads, span),
        compiler_params=pltpu.CompilerParams(
            collective_id=0, has_side_effects=True, vmem_limit_bytes=60 * 1024 * 1024
        ),
        name="attend_project",
    )(span_order, document.reshape(slots, 1, span), queries, keys, values, out_weight)


def gather_attend(queries, keys, values, span_order, document, n_ctx, kv_heads, first_of):
    slots = span_order.shape[0]
    span = document.shape[0] // slots
    rows, depth = queries.shape
    hbm = pl.BlockSpec(memory_space=pl.ANY)
    vmem = pl.BlockSpec(memory_space=pltpu.VMEM)
    return pl.pallas_call(
        functools.partial(gather_attend_kernel, n_ctx, kv_heads, first_of),
        out_shape=jax.ShapeDtypeStruct(queries.shape, queries.dtype),
        in_specs=[pl.BlockSpec(memory_space=pltpu.SMEM), vmem, hbm, hbm, hbm],
        out_specs=vmem,
        scratch_shapes=attention_scratch(n_ctx, rows, depth // HEAD_DIM, kv_heads, span),
        compiler_params=pltpu.CompilerParams(collective_id=0, has_side_effects=True),
        name="gather_attend",
    )(span_order, document.reshape(slots, 1, span), queries, keys, values)


def shards(n_ctx, n_grp, queries, keys, values, out_weight, span_order, document):
    local_heads = queries.shape[1] // HEAD_DIM
    kv_heads = max(1, local_heads // QUERY_GROUP)

    def first_of(group):
        return group * local_heads // QUERY_GROUP

    if n_grp == 4:
        return fused(
            queries, keys, values, out_weight, span_order, document, n_ctx, kv_heads, first_of
        )
    attended = gather_attend(
        queries, keys, values, span_order, document, n_ctx, kv_heads, first_of
    )
    partial_value = jnp.dot(attended, out_weight, preferred_element_type=jnp.float32)
    return lax.psum_scatter(
        partial_value.astype(jnp.bfloat16), "grp", scatter_dimension=1, tiled=True
    )


def solution(mesh):
    in_specs = (P("ctx", "grp"), P("ctx", None), P("ctx", None), P("grp", None), P(), P())
    body = functools.partial(shards, mesh.shape["ctx"], mesh.shape["grp"])
    return jax.shard_map(
        body, mesh=mesh, in_specs=in_specs, out_specs=P("ctx", "grp"), check_vma=False
    )
```

time: 74.7 us -> 72.1 us (0.965)
  Pallas kernels: 72.1 us -> 69.6 us
    pallas_call x2 -> x1, Pallas kernels: 72.1 us -> 69.6 us  [fused(): pl.pallas_call(functools.partial(fused_kernel, n_ctx, kv_heads, first_of)...]
where the time goes in v1:
time: 72.1 us; the launch traced here: 71.9 us
  Pallas kernels  69.6 us (97%)
  local copies, waits for them, and re-layouts  2.3 us (3%)
    pallas_call x1, Pallas kernels, fused(): pl.pallas_call(functools.partial(fused_kernel, n_ctx, kv_heads, first_of)...  69.6 us
    unnamed x1, local copies, waits for them, and re-layouts  2.3 us

profile of v1, /device:TPU:0, one launch (start us, length us, event | category | flops | bytes accessed | tf_op | source)
XLA Modules:
  0.0 71.9 jit_solution(10884177683762850939)
XLA Ops:
  0.0 69.6 %attend_project.1 = bf16[256,2048]{1,0:T(8,128)(2,1)} custom-call(s32[16]{0:T(128)} %order_ref.1, s32[16,1,128]{2,1,0:T(1,128)} %bitcast.1, bf16[256,2048]{1,0:T(8,128)(2,1)} %q_hbm.1, bf16[256,1024]{1,0:T(8,128)(2,1)} %k_hbm.1, bf16[256,1024]{1,0:T(8,128)(2,1)} %v_hbm.1, bf16[2048,8192]{1,0:T(8,128)(2,1)} %w_hbm.1), custom_call_target="tpu_custom_call" | custom-call | tf_op jit(solution)/shard_map/attend_project/pallas_call | solution.py:415
  69.6 2.3 %copy.8 = bf16[256,2048]{1,0:T(8,128)(2,1)} copy(bf16[256,2048]{1,0:T(8,128)(2,1)} %attend_project.1) | data formatting | bytes 2097152

commit v2 on v1

--- a/solution.py
+++ b/solution.py
@@ -31,6 +31,7 @@
     spans = tok_rows // span
     shared = q_ref.shape[1] // HEAD_DIM // kv_heads
     unroll = min(UNROLL, shared)
+    groups = shared // unroll
     factor = math.log2(math.e) / math.sqrt(HEAD_DIM)
     keys_per_step = CORES * tok_rows
     parts_of_keys = keys_per_step // HEAD_DIM
@@ -152,64 +153,79 @@
                     seen, 0.0, HIDDEN
                 )
 
-    def attend(chip, h, low, count):
-        def some_heads(at, carry):
-            both = kv_all[pl.ds(chip * CORES, CORES), h].reshape(keys_per_step, 2 * HEAD_DIM)
-            key = both[:, :HEAD_DIM]
-            value = both[:, HEAD_DIM:]
-            value = jnp.concatenate([value, jnp.ones_like(value)], axis=1)
-            picked = [h * shared + at * unroll + u for u in range(unroll)]
-            rows = pl.ds(low, count)
-            asked = jnp.concatenate(
+    def attend(chip, h, at, low, count):
+        rows = pl.ds(low, count)
+        both = kv_all[pl.ds(chip * CORES, CORES), h].reshape(keys_per_step, 2 * HEAD_DIM)
+        key = both[:, :HEAD_DIM]
+        value = both[:, HEAD_DIM:]
+        value = jnp.concatenate([value, jnp.ones_like(value)], axis=1)
+        picked = [h * shared + at * unroll + u for u in range(unroll)]
+        scores = [
+            lax.dot_general(
+                q_ref[rows, pl.ds(pl.multiple_of(head * HEAD_DIM, HEAD_DIM), HEAD_DIM)],
+                key,
+                (((1,), (1,)), ((), ())),
+                preferred_element_type=jnp.float32,
+            )
+            + bias_ref[rows, :]
+            for head in picked
+        ]
+        olds = [max_ref[head, rows] for head in picked]
+        sums = [acc_ref[head, rows] for head in picked]
+        results = []
+        for score, old, total in zip(scores, olds, sums):
+            top = jnp.maximum(old, jnp.max(score, axis=1, keepdims=True))
+            rescale = jnp.exp2((old - top) * factor)
+            probs = jnp.concatenate(
                 [
-                    q_ref[rows, pl.ds(pl.multiple_of(head * HEAD_DIM, HEAD_DIM), HEAD_DIM)]
-                    for head in picked
+                    jnp.exp2(
+                        (score[:, c * HEAD_DIM : (c + 1) * HEAD_DIM] - top) * factor
+                    ).astype(jnp.bfloat16)
+                    for c in range(parts_of_keys)
                 ],
-                axis=0,
+                axis=1,
             )
-            scores = lax.dot_general(
-                asked, key, (((1,), (1,)), ((), ())), preferred_element_type=jnp.float32
-            )
-            bias = bias_ref[rows, :]
-            tops, rescales, probs = [], [], []
-            for u, head in enumerate(picked):
-                score = scores[u * count : (u + 1) * count] + bias
-                old = max_ref[head, rows]
-                top = jnp.maximum(old, jnp.max(score, axis=1, keepdims=True))
-                tops.append(top)
-                rescales.append(jnp.exp2((old - top) * factor))
-                probs.append(
-                    jnp.concatenate(
-                        [
-                            jnp.exp2(
-                                (score[:, c * HEAD_DIM : (c + 1) * HEAD_DIM] - top) * factor
-                            ).astype(jnp.bfloat16)
-                            for c in range(parts_of_keys)
-                        ],
-                        axis=1,
-                    )
-                )
-            mixed = jnp.dot(
-                jnp.concatenate(probs, axis=0), value, preferred_element_type=jnp.float32
-            )
-            for u, head in enumerate(picked):
-                max_ref[head, rows] = tops[u]
-                scale = jnp.concatenate([rescales[u], rescales[u]], axis=1)
-                acc_ref[head, rows] = (
-                    acc_ref[head, rows] * scale + mixed[u * count : (u + 1) * count]
-                )
+            mixed = jnp.dot(probs, value, preferred_element_type=jnp.float32)
+            scale = jnp.concatenate([rescale, rescale], axis=1)
+            results.append((top, total * scale + mixed))
+        for head, (top, total) in zip(picked, results):
+            max_ref[head, rows] = top
+            acc_ref[head, rows] = total
+
+    def attend_many(chip, h, first, stop, low, count):
+        def one(at, carry):
+            attend(chip, h, at, low, count)
             return carry
 
-        lax.fori_loop(0, shared // unroll, some_heads, 0)
-
-    def step(n, carry):
-        chip = chip_of(n)
-        look(chip)
-        for h in range(kv_heads):
+        lax.fori_loop(first, stop, one, 0)
+
+    def take(k, early):
+        n, h = k // kv_heads, k % kv_heads
+        before = k - 1
+        with jax.named_scope("pass_on"):
             pass_on(n, h)
-            arrived(h, chip, 1 - core)
-            attend(chip, h, 0, tok_rows)
-        return carry
+        with jax.named_scope("rest"):
+            attend_many(chip_of(before // kv_heads), before % kv_heads, early, groups, 0, tok_rows)
+
+        @pl.when(h == 0)
+        def _():
+            look(chip_of(n))
+
+        with jax.named_scope("arrive"):
+            arrived(h, chip_of(n), 1 - core)
+
+    def steps(early, stop):
+        look(z)
+        arrived(0, z, 1 - core)
+        attend_many(z, 0, 0, early, 0, tok_rows)
+
+        def one(k, carry):
+            take(k, early)
+            with jax.named_scope("attend"):
+                attend_many(chip_of(k // kv_heads), k % kv_heads, 0, early, 0, tok_rows)
+            return carry
+
+        lax.fori_loop(1, stop, one, 0)
 
     def result(head, low, count):
         total = acc_ref[head, pl.ds(low, count)]
@@ -254,7 +270,7 @@
     )
     part.start()
     part.prepare()
-    lax.fori_loop(0, part.nz, part.step, 0)
+    part.steps(part.groups, part.nz * kv_heads)
     rows, width = out_ref.shape
     for head in range(width // HEAD_DIM):
         out_ref[:, head * HEAD_DIM : (head + 1) * HEAD_DIM] = part.result(head, 0, rows)
@@ -364,42 +380,52 @@
                 head, r * span, span
             )
 
-    part.start()
+    with jax.named_scope("begin"):
+        part.start()
     for i in range(pieces):
         fetch(i, block_of(i), path_sub(i)[1]).start()
-    part.prepare()
-    lax.fori_loop(0, part.nz - 1, part.step, 0)
-
-    n = part.nz - 1
-    chip = part.chip_of(n)
-    part.look(chip)
-    for h in range(kv_heads - 1):
-        part.pass_on(n, h)
-        part.arrived(h, chip, 1 - part.core)
-        part.attend(chip, h, 0, spans * span)
-    part.pass_on(n, kv_heads - 1)
-    part.arrived(kv_heads - 1, chip, 1 - part.core)
-    part.attend(chip, kv_heads - 1, 0, span)
-    normalise(0)
-    first(0, 0, 8)
-    part.attend(chip, kv_heads - 1, span, span)
-    normalise(1)
-    first(1, 0, 4)
-    second(0)
-    first(1, 4, 8)
-    third(0)
-    second(1)
-    third(1)
-    add_first(0)
-    last(0)
-    add_first(1)
-    last(1)
-    for r in range(spans):
-        for i in range(8):
-            stage_one(r, i).wait_send()
-        for j in range(4):
-            stage_two(r, j).wait_send()
-    part.drain()
+    with jax.named_scope("prepare"):
+        part.prepare()
+    final = part.nz * kv_heads - 1
+    early = (part.groups + 1) // 2
+    part.steps(early, final)
+    part.take(final, early)
+    chip = part.chip_of(part.nz - 1)
+    with jax.named_scope("attend_last"):
+        part.attend_many(chip, kv_heads - 1, 0, part.groups, 0, span)
+        normalise(0)
+    with jax.named_scope("first_0"):
+        first(0, 0, 8)
+    with jax.named_scope("attend_1"):
+        part.attend_many(chip, kv_heads - 1, 0, part.groups, span, span)
+        normalise(1)
+    with jax.named_scope("first_1_far"):
+        first(1, 0, 4)
+    with jax.named_scope("second_0"):
+        second(0)
+    with jax.named_scope("first_1_near"):
+        first(1, 4, 8)
+    with jax.named_scope("third_0"):
+        third(0)
+    with jax.named_scope("second_1"):
+        second(1)
+    with jax.named_scope("third_1"):
+        third(1)
+    with jax.named_scope("add_0"):
+        add_first(0)
+    with jax.named_scope("last_0"):
+        last(0)
+    with jax.named_scope("add_1"):
+        add_first(1)
+    with jax.named_scope("last_1"):
+        last(1)
+    with jax.named_scope("drain"):
+        for r in range(spans):
+            for i in range(8):
+                stage_one(r, i).wait_send()
+            for j in range(4):
+                stage_two(r, j).wait_send()
+        part.drain()
 
 
 def fused(queries, keys, values, out_weight, span_order, document, n_ctx, kv_heads, first_of):
@@ -414,7 +440,7 @@
     vmem = pl.BlockSpec(memory_space=pltpu.VMEM)
     return pl.pallas_call(
         functools.partial(fused_kernel, n_ctx, kv_heads, first_of),
-        out_shape=jax.ShapeDtypeStruct((rows, features // 4), bf16),
+        out_shape=pltpu.VMEM((rows, features // 4), bf16),
         in_specs=[pl.BlockSpec(memory_space=pltpu.SMEM), vmem, hbm, hbm, hbm, hbm],
         out_specs=vmem,
         scratch_shapes=[

time: 72.1 us -> 65 us (0.902)
  Pallas kernels: 69.6 us -> 63.8 us
  local copies, waits for them, and re-layouts: 2.3 us -> 0.97 us
    pallas_call x1, Pallas kernels: 69.6 us -> 63.8 us  [fused(): pl.pallas_call(functools.partial(fused_kernel, n_ctx, kv_heads, first_of)...]
    unnamed x1, local copies, waits for them, and re-layouts: 2.3 us -> 0.97 us
where the time goes in v2:
time: 65 us; the launch traced here: 64.8 us
  Pallas kernels  63.8 us (98%)
  local copies, waits for them, and re-layouts  0.97 us (1%)
    pallas_call x1, Pallas kernels, fused(): pl.pallas_call(functools.partial(fused_kernel, n_ctx, kv_heads, first_of)...  63.8 us

profile of v2, /device:TPU:0, one launch (start us, length us, event | category | flops | bytes accessed | tf_op | source)
XLA Modules:
  0.0 64.8 jit_solution(9302192911595482369)
XLA Ops:
  0.0 63.8 %attend_project.1 = bf16[256,2048]{1,0:T(8,128)(2,1)S(1)} custom-call(s32[16]{0:T(128)} %order_ref.1, s32[16,1,128]{2,1,0:T(1,128)} %bitcast.1, bf16[256,2048]{1,0:T(8,128)(2,1)} %q_hbm.1, bf16[256,1024]{1,0:T(8,128)(2,1)} %k_hbm.1, bf16[256,1024]{1,0:T(8,128)(2,1)} %v_hbm.1, bf16[2048,8192]{1,0:T(8,128)(2,1)} %w_hbm.1), custom_call_target="tpu_custom_call" | custom-call | tf_op jit(solution)/shard_map/attend_project/pallas_call | solution.py:441
  63.8 1.0 %copy.8 = bf16[256,2048]{1,0:T(8,128)(2,1)} copy(bf16[256,2048]{1,0:T(8,128)(2,1)S(1)} %attend_project.1) | data formatting | bytes 2097152

commit v3 on v2

--- a/solution.py
+++ b/solution.py
@@ -18,8 +18,9 @@
 
 
 def attention(
-    n_ctx, kv_heads, first_of, greeted, order_ref, doc_rows, q_hbm, k_hbm, v_hbm,
-    q_ref, kv_all, row_doc_ref, bias_ref, max_ref, acc_ref, local_sem, send_sem, recv_sem,
+    n_ctx, kv_heads, first_of, greeted, order_hbm, doc_hbm, q_hbm, k_hbm, v_hbm,
+    order_ref, doc_rows, q_ref, kv_all, row_doc_ref, bias_ref, max_ref, acc_ref,
+    local_sem, send_sem, recv_sem,
 ):
     nz = n_ctx // CORES
     me = lax.axis_index("ctx")
@@ -43,7 +44,7 @@
         return pltpu.make_async_remote_copy(
             src_ref=kv_all.at[block, h],
             dst_ref=kv_all.at[block, h],
-            send_sem=send_sem.at[way, h, chip],
+            send_sem=send_sem.at[way // 2],
             recv_sem=recv_sem.at[h, block],
             device_id=(target, group),
             device_id_type=MESH,
@@ -60,15 +61,22 @@
         return pltpu.make_async_copy(
             (k_hbm, v_hbm)[side].at[:, pl.ds(start, HEAD_DIM)],
             kv_all.at[me, h, :, pl.ds(side * HEAD_DIM, HEAD_DIM)],
-            local_sem.at[h, side],
+            local_sem.at[h],
         )
 
-    q_load = pltpu.make_async_copy(q_hbm, q_ref, local_sem.at[kv_heads, 0])
+    def loaded(h):
+        pltpu.make_async_copy(kv_all.at[me, h], kv_all.at[me, h], local_sem.at[h]).wait()
+
+    q_load = pltpu.make_async_copy(q_hbm, q_ref, local_sem.at[kv_heads])
+    order_load = pltpu.make_async_copy(order_hbm, order_ref, local_sem.at[kv_heads + 1])
+    doc_load = pltpu.make_async_copy(doc_hbm, doc_rows, local_sem.at[kv_heads + 2])
 
     def start():
         for h in range(kv_heads):
             for side in range(2):
                 load(h, side).start()
+        order_load.start()
+        doc_load.start()
         q_load.start()
         barrier = pltpu.get_barrier_semaphore()
         for target in [(partner, group)] + greeted:
@@ -90,8 +98,7 @@
             barrier, 1 + len(greeted) + jnp.minimum(z, 1) + jnp.minimum(nz - 1 - z, 1)
         )
         for h in range(kv_heads):
-            for side in range(2):
-                load(h, side).wait()
+            loaded(h)
 
             @pl.when(z < nz - 1)
             def _():
@@ -106,6 +113,8 @@
     def prepare():
         max_ref[...] = jnp.full(max_ref.shape, HIDDEN, jnp.float32)
         acc_ref[...] = jnp.zeros(acc_ref.shape, jnp.float32)
+        order_load.wait()
+        doc_load.wait()
         for r in range(spans):
             row_doc_ref[r] = jnp.transpose(
                 jnp.broadcast_to(doc_rows[order_ref[me * spans + r]], (span, span))
@@ -232,41 +241,40 @@
         return (total[:, :HEAD_DIM] / total[:, HEAD_DIM:]).astype(jnp.bfloat16)
 
     def drain():
-        for h in range(kv_heads):
-            for chip in range(nz):
-                piece(2, h, chip, partner).wait_send()
-
-                @pl.when((z < nz - 1) & (chip <= z))
-                def _():
-                    piece(0, h, chip, me + CORES).wait_send()
-
-                @pl.when((z > 0) & (chip >= z))
-                def _():
-                    piece(1, h, chip, me - CORES).wait_send()
+        pltpu.make_async_copy(kv_all.at[:nz], kv_all.at[:nz], send_sem.at[1]).wait()
+        for at in range(nz):
+            sent = (at + 1) * (at < nz - 1) + (nz - at) * (at > 0)
+
+            @pl.when(z == at)
+            def _():
+                blocks = kv_all.at[:sent]
+                pltpu.make_async_copy(blocks, blocks, send_sem.at[0]).wait()
 
     return SimpleNamespace(**locals())
 
 
-def attention_scratch(n_ctx, rows, heads, kv_heads, span):
+def attention_scratch(n_ctx, slots, rows, heads, kv_heads, span):
     f32, bf16 = jnp.float32, jnp.bfloat16
     return [
+        pltpu.SMEM((slots,), jnp.int32),
+        pltpu.VMEM((slots, 1, span), jnp.int32),
         pltpu.VMEM((rows, heads * HEAD_DIM), bf16),
         pltpu.VMEM((n_ctx, kv_heads, rows, 2 * HEAD_DIM), bf16),
         pltpu.VMEM((rows // span, span, span), jnp.int32),
         pltpu.VMEM((rows, CORES * rows), f32),
         pltpu.VMEM((heads, rows, HEAD_DIM), f32),
         pltpu.VMEM((heads, rows, 2 * HEAD_DIM), f32),
-        pltpu.SemaphoreType.DMA((kv_heads + 1, 2)),
-        pltpu.SemaphoreType.DMA((3, kv_heads, n_ctx // CORES)),
+        pltpu.SemaphoreType.DMA((kv_heads + 3,)),
+        pltpu.SemaphoreType.DMA((2,)),
         pltpu.SemaphoreType.DMA((kv_heads, n_ctx)),
     ]
 
 
 def gather_attend_kernel(
-    n_ctx, kv_heads, first_of, order_ref, doc_rows, q_hbm, k_hbm, v_hbm, out_ref, *scratch
+    n_ctx, kv_heads, first_of, order_hbm, doc_hbm, q_hbm, k_hbm, v_hbm, out_ref, *scratch
 ):
     part = attention(
-        n_ctx, kv_heads, first_of, [], order_ref, doc_rows, q_hbm, k_hbm, v_hbm, *scratch
+        n_ctx, kv_heads, first_of, [], order_hbm, doc_hbm, q_hbm, k_hbm, v_hbm, *scratch
     )
     part.start()
     part.prepare()
@@ -278,9 +286,9 @@
 
 
 def fused_kernel(
-    n_ctx, kv_heads, first_of, order_ref, doc_rows, q_hbm, k_hbm, v_hbm, w_hbm, out_ref,
-    att_ref, w_buf, send_one, got_one, send_two, got_two, own_ref,
-    w_sem, sent_one, recv_one, sent_two, recv_two, *scratch,
+    n_ctx, kv_heads, first_of, order_hbm, doc_hbm, q_hbm, k_hbm, v_hbm, w_hbm, out_ref,
+    att_ref, w_buf, send_ref, got_ref, own_ref,
+    w_sem, sent_sem, far_sem, near_sem, two_sem, *scratch,
 ):
     me = lax.axis_index("ctx")
     group = lax.axis_index("grp")
@@ -291,9 +299,9 @@
     block_width = out_ref.shape[1]
     part = attention(
         n_ctx, kv_heads, first_of, [(me, side), (me, other)],
-        order_ref, doc_rows, q_hbm, k_hbm, v_hbm, *scratch,
+        order_hbm, doc_hbm, q_hbm, k_hbm, v_hbm, *scratch,
     )
-    span, spans = part.span, part.spans
+    spans, span = att_ref.shape[:2]
     heads = part.q_ref.shape[1] // HEAD_DIM
 
     def path_sub(i):
@@ -307,52 +315,58 @@
 
     def fetch(i, block, sub):
         start = pl.multiple_of(block * block_width + sub * width, width)
-        return pltpu.make_async_copy(w_hbm.at[:, pl.ds(start, width)], w_buf.at[i], w_sem.at[i])
+        return pltpu.make_async_copy(
+            w_hbm.at[:, pl.ds(start, width)], w_buf.at[i], w_sem.at[i // 8]
+        )
+
+    def fetched(half):
+        part_of = w_buf.at[pl.ds(half * 8, 8)]
+        pltpu.make_async_copy(part_of, part_of, w_sem.at[half]).wait()
 
     def product(r, i):
-        if r == 0:
-            fetch(i, group, 0).wait()
         return jnp.dot(att_ref[r], w_buf[i], preferred_element_type=jnp.float32)
 
-    def stage_one(r, i):
-        path = i % 2
+    def send(r, i, path, sem):
         return pltpu.make_async_remote_copy(
-            src_ref=send_one.at[r, i],
-            dst_ref=got_one.at[r, i],
-            send_sem=sent_one.at[r, i],
-            recv_sem=recv_one.at[r, i],
+            src_ref=send_ref.at[r, i],
+            dst_ref=got_ref.at[r, i],
+            send_sem=sent_sem.at[0],
+            recv_sem=sem,
             device_id=(me, (1 - path) * side + path * other),
             device_id_type=MESH,
         )
 
-    def stage_two(r, j):
-        path = j % 2
-        return pltpu.make_async_remote_copy(
-            src_ref=send_two.at[r, j],
-            dst_ref=got_two.at[r, j],
-            send_sem=sent_two.at[r, j],
-            recv_sem=recv_two.at[r, j],
-            device_id=(me, (1 - path) * other + path * side),
-            device_id_type=MESH,
-        )
-
-    def first(r, low, high):
+    def got(r, low, count, sem):
+        part_of = got_ref.at[r, pl.ds(low, count)]
+        pltpu.make_async_copy(part_of, part_of, sem).wait()
+
+    def first_far(r):
         def one(i, carry):
-            send_one[r, i] = product(r, i).astype(send_one.dtype)
-            stage_one(r, i).start()
+            send_ref[r, i] = product(r, i).astype(send_ref.dtype)
+            send(r, i, i % 2, far_sem.at[r, i]).start()
             return carry
 
-        lax.fori_loop(low, high, one, 0)
+        lax.fori_loop(0, 4, one, 0)
+
+    def first_near(r):
+        def one(i, carry):
+            send_ref[r, i] = product(r, i).astype(send_ref.dtype)
+            send(r, i, i % 2, near_sem.at[r]).start()
+            return carry
+
+        lax.fori_loop(4, 8, one, 0)
 
     def second(r):
-        def one(j, carry):
-            value = product(r, 8 + j)
-            stage_one(r, j).wait_recv()
-            send_two[r, j] = (value + got_one[r, j].astype(jnp.float32)).astype(send_two.dtype)
-            stage_two(r, j).start()
+        def one(i, carry):
+            value = product(r, i)
+            got(r, i - 8, 1, far_sem.at[r, i - 8])
+            send_ref[r, i] = (value + got_ref[r, i - 8].astype(jnp.float32)).astype(
+                send_ref.dtype
+            )
+            send(r, i, 1 - i % 2, two_sem.at[r, i - 8]).start()
             return carry
 
-        lax.fori_loop(0, 4, one, 0)
+        lax.fori_loop(8, 12, one, 0)
 
     def third(r):
         def one(j, carry):
@@ -362,20 +376,20 @@
         lax.fori_loop(0, 4, one, 0)
 
     def add_first(r):
+        got(r, 4, 4, near_sem.at[r])
         for j in range(4):
-            stage_one(r, 4 + j).wait_recv()
-            own_ref[r, j] = own_ref[r, j] + got_one[r, 4 + j].astype(jnp.float32)
+            own_ref[r, j] = own_ref[r, j] + got_ref[r, 4 + j].astype(jnp.float32)
 
     def last(r):
         for j in range(4):
-            stage_two(r, j).wait_recv()
+            got(r, 8 + j, 1, two_sem.at[r, j])
             at = path_sub(j)[1] * width
             out_ref[r * span : (r + 1) * span, at : at + width] = (
-                own_ref[r, j] + got_two[r, j].astype(jnp.float32)
+                own_ref[r, j] + got_ref[r, 8 + j].astype(jnp.float32)
             ).astype(out_ref.dtype)
 
-    def normalise(r):
-        for head in range(heads):
+    def normalise(r, first, stop):
+        for head in range(first, stop):
             att_ref[r, :, head * HEAD_DIM : (head + 1) * HEAD_DIM] = part.result(
                 head, r * span, span
             )
@@ -388,23 +402,28 @@
         part.prepare()
     final = part.nz * kv_heads - 1
     early = (part.groups + 1) // 2
+    done = (kv_heads - 1) * part.shared
     part.steps(early, final)
     part.take(final, early)
     chip = part.chip_of(part.nz - 1)
     with jax.named_scope("attend_last"):
         part.attend_many(chip, kv_heads - 1, 0, part.groups, 0, span)
-        normalise(0)
+    with jax.named_scope("norm"):
+        normalise(0, 0, heads)
     with jax.named_scope("first_0"):
-        first(0, 0, 8)
+        fetched(0)
+        first_far(0)
+        first_near(0)
     with jax.named_scope("attend_1"):
         part.attend_many(chip, kv_heads - 1, 0, part.groups, span, span)
-        normalise(1)
+        normalise(1, 0, heads)
     with jax.named_scope("first_1_far"):
-        first(1, 0, 4)
+        first_far(1)
+        fetched(1)
     with jax.named_scope("second_0"):
         second(0)
     with jax.named_scope("first_1_near"):
-        first(1, 4, 8)
+        first_near(1)
     with jax.named_scope("third_0"):
         third(0)
     with jax.named_scope("second_1"):
@@ -420,11 +439,7 @@
     with jax.named_scope("last_1"):
         last(1)
     with jax.named_scope("drain"):
-        for r in range(spans):
-            for i in range(8):
-                stage_one(r, i).wait_send()
-            for j in range(4):
-                stage_two(r, j).wait_send()
+        pltpu.make_async_copy(send_ref, send_ref, sent_sem.at[0]).wait()
         part.drain()
 
 
@@ -441,23 +456,21 @@
     return pl.pallas_call(
         functools.partial(fused_kernel, n_ctx, kv_heads, first_of),
         out_shape=pltpu.VMEM((rows, features // 4), bf16),
-        in_specs=[pl.BlockSpec(memory_space=pltpu.SMEM), vmem, hbm, hbm, hbm, hbm],
+        in_specs=[hbm] * 6,
         out_specs=vmem,
         scratch_shapes=[
             pltpu.VMEM((spans, span, depth), bf16),
             pltpu.VMEM((16, depth, width), bf16),
-            pltpu.VMEM((spans, 8, span, width), bf16),
-            pltpu.VMEM((spans, 8, span, width), bf16),
-            pltpu.VMEM((spans, 4, span, width), bf16),
-            pltpu.VMEM((spans, 4, span, width), bf16),
+            pltpu.VMEM((spans, 12, span, width), bf16),
+            pltpu.VMEM((spans, 12, span, width), bf16),
             pltpu.VMEM((spans, 4, span, width), f32),
-            pltpu.SemaphoreType.DMA((16,)),
-            pltpu.SemaphoreType.DMA((spans, 8)),
-            pltpu.SemaphoreType.DMA((spans, 8)),
+            pltpu.SemaphoreType.DMA((2,)),
+            pltpu.SemaphoreType.DMA((1,)),
             pltpu.SemaphoreType.DMA((spans, 4)),
+            pltpu.SemaphoreType.DMA((spans,)),
             pltpu.SemaphoreType.DMA((spans, 4)),
         ]
-        + attention_scratch(n_ctx, rows, depth // HEAD_DIM, kv_heads, span),
+        + attention_scratch(n_ctx, slots, rows, depth // HEAD_DIM, kv_heads, span),
         compiler_params=pltpu.CompilerParams(
             collective_id=0, has_side_effects=True, vmem_limit_bytes=60 * 1024 * 1024
         ),
@@ -474,9 +487,9 @@
     return pl.pallas_call(
         functools.partial(gather_attend_kernel, n_ctx, kv_heads, first_of),
         out_shape=jax.ShapeDtypeStruct(queries.shape, queries.dtype),
-        in_specs=[pl.BlockSpec(memory_space=pltpu.SMEM), vmem, hbm, hbm, hbm],
+        in_specs=[hbm] * 5,
         out_specs=vmem,
-        scratch_shapes=attention_scratch(n_ctx, rows, depth // HEAD_DIM, kv_heads, span),
+        scratch_shapes=attention_scratch(n_ctx, slots, rows, depth // HEAD_DIM, kv_heads, span),
         compiler_params=pltpu.CompilerParams(collective_id=0, has_side_effects=True),
         name="gather_attend",
     )(span_order, document.reshape(slots, 1, span), queries, keys, values)

time: 65 us -> 63.4 us (0.975)
  Pallas kernels: 63.8 us -> 62.2 us
    pallas_call x1, Pallas kernels: 63.8 us -> 62.2 us  [fused(): pl.pallas_call(functools.partial(fused_kernel, n_ctx, kv_heads, first_of)...]
where the time goes in v3:
time: 63.4 us; the launch traced here: 63.2 us
  Pallas kernels  62.2 us (98%)
  local copies, waits for them, and re-layouts  0.97 us (2%)
    pallas_call x1, Pallas kernels, fused(): pl.pallas_call(functools.partial(fused_kernel, n_ctx, kv_heads, first_of)...  62.2 us

profile of v3, /device:TPU:0, one launch (start us, length us, event | category | flops | bytes accessed | tf_op | source)
XLA Modules:
  0.0 63.2 jit_solution(7972716543652185346)
XLA Ops:
  0.0 62.2 %attend_project.1 = bf16[256,2048]{1,0:T(8,128)(2,1)S(1)} custom-call(s32[16]{0:T(128)} %order_hbm.1, s32[16,1,128]{2,1,0:T(1,128)} %bitcast.1, bf16[256,2048]{1,0:T(8,128)(2,1)} %q_hbm.1, bf16[256,1024]{1,0:T(8,128)(2,1)} %k_hbm.1, bf16[256,1024]{1,0:T(8,128)(2,1)} %v_hbm.1, bf16[2048,8192]{1,0:T(8,128)(2,1)} %w_hbm.1), custom_call_target="tpu_custom_call" | custom-call | tf_op jit(solution)/shard_map/attend_project/pallas_call | solution.py:456
  62.2 1.0 %copy.8 = bf16[256,2048]{1,0:T(8,128)(2,1)} copy(bf16[256,2048]{1,0:T(8,128)(2,1)S(1)} %attend_project.1) | data formatting | bytes 2097152

commit v4 on v3

v4 whole, which is shorter than its diff:
```python
import functools
import math
from types import SimpleNamespace

import jax
import jax.numpy as jnp
from jax import lax
from jax.experimental import pallas as pl
from jax.experimental.pallas import tpu as pltpu
from jax.sharding import PartitionSpec as P

HEAD_DIM = 128
QUERY_GROUP = 8
CORES = 2
MESH = pl.DeviceIdType.MESH
HIDDEN = -1e30
ONES = 16


def attention(
    n_ctx, kv_heads, first_of, greeted, order_hbm, doc_hbm, q_hbm, k_hbm, v_hbm,
    order_ref, doc_rows, q_ref, kv_all, turned_ref, doc_cols, bias_ref, max_ref, acc_ref,
    local_sem, send_sem, recv_sem,
    few_q=None, more_q=None, more_doc=None, more_bias=None, more_max=None, more_acc=None,
    more_sem=None,
):
    nz = n_ctx // CORES
    me = lax.axis_index("ctx")
    group = lax.axis_index("grp")
    z, core = me // CORES, me % CORES
    partner = z * CORES + 1 - core
    tok_rows = kv_all.shape[2]
    span = doc_rows.shape[2]
    spans = tok_rows // span
    shared = q_ref.shape[1] // HEAD_DIM // kv_heads
    factor = math.log2(math.e) / math.sqrt(HEAD_DIM)
    keys_per_step = CORES * tok_rows
    near = jnp.minimum(z, nz - 1 - z)
    extra = HEAD_DIM // shared
    kept = span - extra
    mate = (z + 1 - 2 * (z % 2)) * CORES + core
    long_way = jnp.where(z < nz - 1 - z, 1, -1)

    def piece(way, h, chip, target):
        block = chip * CORES + core
        return pltpu.make_async_remote_copy(
            src_ref=kv_all.at[block, h],
            dst_ref=kv_all.at[block, h],
            send_sem=send_sem.at[way // 2],
            recv_sem=recv_sem.at[h, block],
            device_id=(target, group),
            device_id_type=MESH,
        )

    def arrived(h, chip, from_core):
        block = chip * CORES + from_core
        pltpu.make_async_copy(
            kv_all.at[block, h], kv_all.at[block, h], recv_sem.at[h, block]
        ).wait()

    def load(h, side):
        start = pl.multiple_of((first_of(group) + h) * HEAD_DIM, HEAD_DIM)
        return pltpu.make_async_copy(
            (k_hbm, v_hbm)[side].at[:, pl.ds(start, HEAD_DIM)],
            kv_all.at[me, h, :, pl.ds(side * HEAD_DIM, HEAD_DIM)],
            local_sem.at[h],
        )

    def loaded(h):
        pltpu.make_async_copy(kv_all.at[me, h], kv_all.at[me, h], local_sem.at[h]).wait()

    q_load = pltpu.make_async_copy(q_hbm, q_ref, local_sem.at[kv_heads])
    order_load = pltpu.make_async_copy(order_hbm, order_ref, local_sem.at[kv_heads + 1])
    doc_load = pltpu.make_async_copy(doc_hbm, doc_rows, local_sem.at[kv_heads + 2])

    def lend():
        return pltpu.make_async_remote_copy(
            src_ref=more_q,
            dst_ref=more_q,
            send_sem=more_sem.at[0],
            recv_sem=more_sem.at[1],
            device_id=(mate, group),
            device_id_type=MESH,
        )

    few_load = (
        None if more_q is None else
        pltpu.make_async_copy(q_hbm.at[pl.ds(kept, extra)], few_q, more_sem.at[2])
    )

    def stage():
        for head in range(kv_heads * shared):
            h, u = head // shared, head % shared
            more_q[h, u * extra : (u + 1) * extra] = few_q[
                :, head * HEAD_DIM : (head + 1) * HEAD_DIM
            ]
        lend().start()

    def start():
        for h in range(kv_heads):
            for side in range(2):
                load(h, side).start()
        order_load.start()
        doc_load.start()
        if few_load is not None:
            few_load.start()
        q_load.start()
        barrier = pltpu.get_barrier_semaphore()
        for target in [(partner, group)] + greeted:
            pl.semaphore_signal(barrier, inc=1, device_id=target, device_id_type=MESH)

        @pl.when(z > 0)
        def _():
            pl.semaphore_signal(
                barrier, inc=1, device_id=(me - CORES, group), device_id_type=MESH
            )

        @pl.when(z < nz - 1)
        def _():
            pl.semaphore_signal(
                barrier, inc=1, device_id=(me + CORES, group), device_id_type=MESH
            )

        pl.semaphore_wait(
            barrier, 1 + len(greeted) + jnp.minimum(z, 1) + jnp.minimum(nz - 1 - z, 1)
        )
        for h in range(kv_heads):
            loaded(h)

            @pl.when(z < nz - 1)
            def _():
                piece(0, h, z, me + CORES).start()

            @pl.when(z > 0)
            def _():
                piece(1, h, z, me - CORES).start()

            piece(2, h, z, partner).start()
            if h == 0 and few_load is not None:
                few_load.wait()
                pl.when(near == 0)(stage)

    def prepare():
        max_ref[...] = jnp.full(max_ref.shape, HIDDEN, jnp.float32)
        acc_ref[...] = jnp.zeros(acc_ref.shape, jnp.float32)
        order_load.wait()
        doc_load.wait()
        turned_ref[:, HEAD_DIM:] = jnp.ones((kv_heads, ONES, keys_per_step), turned_ref.dtype)
        for at in range(doc_rows.shape[0]):
            doc_cols[at] = jnp.transpose(jnp.broadcast_to(doc_rows[at], (span, span)))
        if more_q is not None:
            more_max[...] = jnp.full(more_max.shape, HIDDEN, jnp.float32)
            more_acc[...] = jnp.zeros(more_acc.shape, jnp.float32)
            theirs = jnp.broadcast_to(doc_rows[lent_span()], more_doc.shape)
            lane = lax.broadcasted_iota(jnp.int32, more_doc.shape, 1)
            rolled = theirs
            for u in range(shared):
                moved = pltpu.roll(theirs, (u * extra - kept) % span, 1)
                rolled = jnp.where(lane // extra == u, moved, rolled)
            more_doc[...] = rolled
        q_load.wait()

    def pass_on(n, h):
        def from_below():
            arrived(h, z - n, core)

            @pl.when(z < nz - 1)
            def _():
                piece(0, h, z - n, me + CORES).start()

            piece(2, h, z - n, partner).start()

        def from_above():
            arrived(h, z + n, core)

            @pl.when(z > 0)
            def _():
                piece(1, h, z + n, me - CORES).start()

            piece(2, h, z + n, partner).start()

        above_first = z < nz - 1 - z
        pl.when((n > 0) & (z + n < nz) & above_first)(from_above)
        pl.when((n > 0) & (z - n >= 0))(from_below)
        pl.when((n > 0) & (z + n < nz) & jnp.logical_not(above_first))(from_above)

    def chip_of(n):
        away = (n + 1) // 2
        paired = z + away * (1 - 2 * (n % 2))
        return jnp.where(n <= 2 * near, paired, z + long_way * (n - near))

    def lent_span():
        return order_ref[jnp.where(near == 1, mate, me) * spans]

    def look(chip):
        key_at = lax.broadcasted_iota(jnp.int32, (span, span), 0)
        row_at = lax.broadcasted_iota(jnp.int32, (span, span), 1)
        for slot in range(spans * CORES):
            key_span = order_ref[chip * (spans * CORES) + slot]
            key_doc = doc_cols[key_span]
            for r in range(spans):
                mine = order_ref[me * spans + r]
                seen = (key_doc == doc_rows[mine]) & (
                    key_span * span + key_at <= mine * span + row_at
                )
                bias_ref[slot * span : (slot + 1) * span, r * span : (r + 1) * span] = jnp.where(
                    seen, 0.0, HIDDEN
                )
            if more_q is not None:
                seen = (key_doc == more_doc[:1]) & (
                    key_span * span + key_at <= lent_span() * span + kept + row_at % extra
                )
                more_bias[slot * span : (slot + 1) * span] = jnp.where(seen, 0.0, HIDDEN)

    def turn(block, blocks, h):
        both = kv_all[pl.ds(block, blocks), h].reshape(blocks * tok_rows, 2 * HEAD_DIM)
        turned_ref[h, :HEAD_DIM] = jnp.transpose(both[:, HEAD_DIM:])

    def attend(chip, h, low, count, own=True, lent=False):
        rows = pl.ds(low, count)
        key = kv_all[pl.ds(chip * CORES, CORES), h].reshape(keys_per_step, 2 * HEAD_DIM)
        key = key[:, :HEAD_DIM]
        asked = []
        if own:
            for u in range(shared):
                head = h * shared + u
                at = pl.ds(pl.multiple_of(head * HEAD_DIM, HEAD_DIM), HEAD_DIM)
                asked.append(
                    (q_ref[rows, at], bias_ref, max_ref.at[head], acc_ref.at[head], rows)
                )
        if lent:
            every = slice(None)
            asked.append((more_q[h], more_bias, more_max.at[h], more_acc.at[h], every))
        scores = [
            lax.dot_general(
                key, query, (((1,), (1,)), ((), ())), preferred_element_type=jnp.float32
            )
            + bias[:, at]
            for query, bias, _, _, at in asked
        ]
        for (_, _, maxes, sums, at), score in zip(asked, scores):
            old = maxes[:, at]
            top = jnp.maximum(old, jnp.max(score, axis=0, keepdims=True))
            rescale = jnp.exp2((old - top) * factor)
            probs = jnp.exp2((score - top) * factor).astype(jnp.bfloat16)
            mixed = jnp.dot(turned_ref[h], probs, preferred_element_type=jnp.float32)
            maxes[:, at] = top
            sums[:, at] = sums[:, at] * rescale + mixed

    def plan(k):
        middle = near == 1
        after = k - 2
        first_n = jnp.where(
            middle, 2 * (after >= 2), (after > 0) * (k + 1) // 2
        )
        first_h = jnp.where(middle, after == 3, (after > 0) * (k + 1) % 2)
        second_n = jnp.where(after == 0, 1, 0)
        chip = jnp.where(
            middle & (after >= 0), chip_of(1 + after % 2), chip_of(k // kv_heads)
        )
        held = jnp.where(middle & (after >= 0), after // 2, k % kv_heads)
        return first_n, first_h.astype(jnp.int32), second_n, chip, held

    def slots(begin, stop, lent):
        def one(k, carry):
            first_n, first_h, second_n, chip, held = plan(k)
            with jax.named_scope("pass_on"):
                pass_on(first_n, first_h)
                pass_on(second_n, 1)
            look(chip)
            with jax.named_scope("arrive"):
                arrived(held, chip, 1 - core)
            turn(chip * CORES, CORES, held)
            with jax.named_scope("attend"):
                attend(chip, held, 0, tok_rows, lent=lent)
            return carry

        lax.fori_loop(begin, stop, one, 0)

    def steps():
        def one(k, carry):
            n, h = k // kv_heads, k % kv_heads
            pass_on(n, h)
            look(chip_of(n))
            arrived(h, chip_of(n), 1 - core)
            turn(chip_of(n) * CORES, CORES, h)
            attend(chip_of(n), h, 0, tok_rows)
            return carry

        lax.fori_loop(0, nz * kv_heads, one, 0)

    def finished(total):
        scale = 1.0 / total[HEAD_DIM : HEAD_DIM + 1]
        return jnp.transpose((total[:HEAD_DIM] * scale).astype(jnp.bfloat16))

    def result(head, low, count):
        return finished(acc_ref[head, :, pl.ds(low, count)])

    def drain():
        pltpu.make_async_copy(kv_all.at[:nz], kv_all.at[:nz], send_sem.at[1]).wait()
        for at in range(nz):
            sent = (at + 1) * (at < nz - 1) + (nz - at) * (at > 0)

            @pl.when(z == at)
            def _():
                blocks = kv_all.at[:sent]
                pltpu.make_async_copy(blocks, blocks, send_sem.at[0]).wait()

    return SimpleNamespace(**locals())


def attention_scratch(n_ctx, slots, rows, heads, kv_heads, span):
    f32, bf16 = jnp.float32, jnp.bfloat16
    return [
        pltpu.SMEM((slots,), jnp.int32),
        pltpu.VMEM((slots, 1, span), jnp.int32),
        pltpu.VMEM((rows, heads * HEAD_DIM), bf16),
        pltpu.VMEM((n_ctx, kv_heads, rows, 2 * HEAD_DIM), bf16),
        pltpu.VMEM((kv_heads, HEAD_DIM + ONES, CORES * rows), bf16),
        pltpu.VMEM((slots, span, span), jnp.int32),
        pltpu.VMEM((CORES * rows, rows), f32),
        pltpu.VMEM((heads, 1, rows), f32),
        pltpu.VMEM((heads, HEAD_DIM + ONES, rows), f32),
        pltpu.SemaphoreType.DMA((kv_heads + 3,)),
        pltpu.SemaphoreType.DMA((2,)),
        pltpu.SemaphoreType.DMA((kv_heads, n_ctx)),
    ]


def gather_attend_kernel(
    n_ctx, kv_heads, first_of, order_hbm, doc_hbm, q_hbm, k_hbm, v_hbm, out_ref, *scratch
):
    part = attention(
        n_ctx, kv_heads, first_of, [], order_hbm, doc_hbm, q_hbm, k_hbm, v_hbm, *scratch
    )
    part.start()
    part.prepare()
    part.steps()
    rows, width = out_ref.shape
    for head in range(width // HEAD_DIM):
        out_ref[:, head * HEAD_DIM : (head + 1) * HEAD_DIM] = part.result(head, 0, rows)
    part.drain()


def fused_kernel(
    n_ctx, kv_heads, first_of, order_hbm, doc_hbm, q_hbm, k_hbm, v_hbm, w_hbm, out_ref,
    att_ref, w_buf, send_ref, got_ref, own_ref, back_out, back_in,
    w_sem, sent_sem, far_sem, near_sem, two_sem, back_sem, *scratch,
):
    me = lax.axis_index("ctx")
    group = lax.axis_index("grp")
    side = group + 1 - 2 * (group % 2)
    other = (group + 2) % 4
    far = 3 - group
    pieces, _, width = w_buf.shape
    block_width = out_ref.shape[1]
    part = attention(
        n_ctx, kv_heads, first_of, [(me, side), (me, other)],
        order_hbm, doc_hbm, q_hbm, k_hbm, v_hbm, *scratch,
    )
    span, spans, extra, kept, shared = part.span, part.spans, part.extra, part.kept, part.shared
    middle = part.near == 1

    def path_sub(i):
        path = i % 2
        return path, 2 * path + (i // 2) % 2

    def block_of(i):
        path = i % 2
        first = far if i < 4 else (other if path else side)
        return first if i < 8 else ((side if path else other) if i < 12 else group)

    def fetch(i, block, sub):
        start = pl.multiple_of(block * block_width + sub * width, width)
        return pltpu.make_async_copy(
            w_hbm.at[:, pl.ds(start, width)], w_buf.at[i], w_sem.at[i // 8]
        )

    def fetched(half):
        part_of = w_buf.at[pl.ds(half * 8, 8)]
        pltpu.make_async_copy(part_of, part_of, w_sem.at[half]).wait()

    def held_rows(r):
        return span if r else span + extra

    def sized(r, do):
        if r:
            do(span)
        else:
            pl.when(middle)(lambda: do(span + extra))
            pl.when(jnp.logical_not(middle))(lambda: do(kept))

    def product(r, i):
        return jnp.dot(
            att_ref[r, : held_rows(r)], w_buf[i], preferred_element_type=jnp.float32
        )

    def send(r, i, path, sem):
        sized(
            r,
            lambda count: pltpu.make_async_remote_copy(
                src_ref=send_ref.at[r, i, :count],
                dst_ref=got_ref.at[r, i, :count],
                send_sem=sent_sem.at[r],
                recv_sem=sem,
                device_id=(me, (1 - path) * side + path * other),
                device_id_type=MESH,
            ).start(),
        )

    def got(r, low, pieces_of, sem):
        def wait(count):
            part_of = got_ref.at[r, pl.ds(low, pieces_of), :count]
            pltpu.make_async_copy(part_of, part_of, sem).wait()

        sized(r, wait)

    def sent(r):
        def wait(count):
            part_of = send_ref.at[r, :, :count]
            pltpu.make_async_copy(part_of, part_of, sent_sem.at[r]).wait()

        sized(r, wait)

    def give_back():
        return pltpu.make_async_remote_copy(
            src_ref=back_out,
            dst_ref=back_in,
            send_sem=back_sem.at[0],
            recv_sem=back_sem.at[1],
            device_id=(part.mate, group),
            device_id_type=MESH,
        )

    def first_far(r):
        def one(i, carry):
            send_ref[r, i, : held_rows(r)] = product(r, i).astype(send_ref.dtype)
            send(r, i, i % 2, far_sem.at[r, i])
            return carry

        lax.fori_loop(0, 4, one, 0)

    def first_near(r):
        def one(i, carry):
            send_ref[r, i, : held_rows(r)] = product(r, i).astype(send_ref.dtype)
            send(r, i, i % 2, near_sem.at[r])
            return carry

        lax.fori_loop(4, 8, one, 0)

    def second(r):
        def one(i, carry):
            value = product(r, i)
            got(r, i - 8, 1, far_sem.at[r, i - 8])
            count = held_rows(r)
            send_ref[r, i, :count] = (
                value + got_ref[r, i - 8, :count].astype(jnp.float32)
            ).astype(send_ref.dtype)
            send(r, i, 1 - i % 2, two_sem.at[r, i - 8])
            return carry

        lax.fori_loop(8, 12, one, 0)

    def third(r):
        def one(j, carry):
            own_ref[r, j, : held_rows(r)] = product(r, 12 + j)
            return carry

        lax.fori_loop(0, 4, one, 0)

    def add_first(r):
        got(r, 4, 4, near_sem.at[r])
        for j in range(4):
            count = held_rows(r)
            own_ref[r, j, :count] = own_ref[r, j, :count] + got_ref[r, 4 + j, :count].astype(
                jnp.float32
            )

    def last(r):
        for j in range(4):
            got(r, 8 + j, 1, two_sem.at[r, j])
            at = path_sub(j)[1] * width
            total = (
                own_ref[r, j, : held_rows(r)]
                + got_ref[r, 8 + j, : held_rows(r)].astype(jnp.float32)
            ).astype(out_ref.dtype)
            if r:
                out_ref[span:, at : at + width] = total
            else:
                out_ref[:kept, at : at + width] = total[:kept]

                @pl.when(middle)
                def _():
                    out_ref[kept:span, at : at + width] = total[kept:span]
                    back_out[:, at : at + width] = total[span:]

    def normalise(r, h):
        for head in range(h * shared, (h + 1) * shared):
            att_ref[r, :span, head * HEAD_DIM : (head + 1) * HEAD_DIM] = part.result(
                head, r * span, span
            )
        if r == 0:
            lent = part.finished(part.more_acc[h])
            for u in range(shared):
                at = (h * shared + u) * HEAD_DIM
                att_ref[0, span:, at : at + HEAD_DIM] = lent[u * extra : (u + 1) * extra]

    with jax.named_scope("begin"):
        part.start()
    for i in range(pieces):
        fetch(i, block_of(i), path_sub(i)[1]).start()
    with jax.named_scope("prepare"):
        part.prepare()
    part.slots(0, 2, False)
    with jax.named_scope("pass_on"):
        part.pass_on(1, 0)
    with jax.named_scope("lent"):
        pl.when(middle)(lambda: part.lend().wait_recv())
        for h in range(kv_heads):
            part.attend(part.z, h, 0, 0, own=False, lent=True)
    part.slots(2, 6, True)
    chip = part.chip_of(3)
    with jax.named_scope("pass_on"):
        part.pass_on(jnp.where(middle, 0, 3), 1)
    part.look(chip)
    for h in range(kv_heads):
        with jax.named_scope("arrive"):
            part.arrived(h, chip, 1 - part.core)
        with jax.named_scope("attend_0"):
            part.turn(chip * CORES, CORES, h)
            part.attend(chip, h, 0, span, lent=True)
        with jax.named_scope("norm"):
            normalise(0, h)
    with jax.named_scope("first_0"):
        fetched(0)
        first_far(0)
        first_near(0)
    with jax.named_scope("attend_1"):
        for h in range(kv_heads):
            part.attend(chip, h, span, span)
            normalise(1, h)
    with jax.named_scope("first_1_far"):
        first_far(1)
        fetched(1)
    with jax.named_scope("second_0"):
        second(0)
    with jax.named_scope("first_1_near"):
        first_near(1)
    with jax.named_scope("third_0"):
        third(0)
    with jax.named_scope("second_1"):
        second(1)
    with jax.named_scope("third_1"):
        third(1)
    with jax.named_scope("add_0"):
        add_first(0)
    with jax.named_scope("last_0"):
        last(0)
        pl.when(middle)(lambda: give_back().start())
    with jax.named_scope("add_1"):
        add_first(1)
    with jax.named_scope("last_1"):
        last(1)
    with jax.named_scope("drain"):
        @pl.when(middle)
        def _():
            give_back().wait_send()

        @pl.when(jnp.logical_not(middle))
        def _():
            give_back().wait_recv()
            out_ref[kept:span] = back_in[...]
            part.lend().wait_send()

        for r in range(spans):
            sent(r)
        part.drain()


def fused(queries, keys, values, out_weight, span_order, document, n_ctx, kv_heads, first_of):
    slots = span_order.shape[0]
    span = document.shape[0] // slots
    rows, depth = queries.shape
    features = out_weight.shape[1]
    width = features // 16
    spans = rows // span
    heads = depth // HEAD_DIM
    extra = HEAD_DIM * kv_heads // heads
    most = span + extra
    f32, bf16 = jnp.float32, jnp.bfloat16
    hbm = pl.BlockSpec(memory_space=pl.ANY)
    vmem = pl.BlockSpec(memory_space=pltpu.VMEM)
    return pl.pallas_call(
        functools.partial(fused_kernel, n_ctx, kv_heads, first_of),
        out_shape=pltpu.VMEM((rows, features // 4), bf16),
        in_specs=[hbm] * 6,
        out_specs=vmem,
        scratch_shapes=[
            pltpu.VMEM((spans, most, depth), bf16),
            pltpu.VMEM((16, depth, width), bf16),
            pltpu.VMEM((spans, 12, most, width), bf16),
            pltpu.VMEM((spans, 12, most, width), bf16),
            pltpu.VMEM((spans, 4, most, width), f32),
            pltpu.VMEM((extra, features // 4), bf16),
            pltpu.VMEM((extra, features // 4), bf16),
            pltpu.SemaphoreType.DMA((2,)),
            pltpu.SemaphoreType.DMA((spans,)),
            pltpu.SemaphoreType.DMA((spans, 4)),
            pltpu.SemaphoreType.DMA((spans,)),
            pltpu.SemaphoreType.DMA((spans, 4)),
            pltpu.SemaphoreType.DMA((2,)),
        ]
        + attention_scratch(n_ctx, slots, rows, heads, kv_heads, span)
        + [
            pltpu.VMEM((extra, depth), bf16),
            pltpu.VMEM((kv_heads, HEAD_DIM, HEAD_DIM), bf16),
            pltpu.VMEM((8, span), jnp.int32),
            pltpu.VMEM((CORES * rows, HEAD_DIM), f32),
            pltpu.VMEM((kv_heads, 1, HEAD_DIM), f32),
            pltpu.VMEM((kv_heads, HEAD_DIM + ONES, HEAD_DIM), f32),
            pltpu.SemaphoreType.DMA((3,)),
        ],
        compiler_params=pltpu.CompilerParams(
            collective_id=0, has_side_effects=True, vmem_limit_bytes=60 * 1024 * 1024
        ),
        name="attend_project",
    )(span_order, document.reshape(slots, 1, span), queries, keys, values, out_weight)


def gather_attend(queries, keys, values, span_order, document, n_ctx, kv_heads, first_of):
    slots = span_order.shape[0]
    span = document.shape[0] // slots
    rows, depth = queries.shape
    hbm = pl.BlockSpec(memory_space=pl.ANY)
    vmem = pl.BlockSpec(memory_space=pltpu.VMEM)
    return pl.pallas_call(
        functools.partial(gather_attend_kernel, n_ctx, kv_heads, first_of),
        out_shape=jax.ShapeDtypeStruct(queries.shape, queries.dtype),
        in_specs=[hbm] * 5,
        out_specs=vmem,
        scratch_shapes=attention_scratch(n_ctx, slots, rows, depth // HEAD_DIM, kv_heads, span),
        compiler_params=pltpu.CompilerParams(collective_id=0, has_side_effects=True),
        name="gather_attend",
    )(span_order, document.reshape(slots, 1, span), queries, keys, values)


def shards(n_ctx, n_grp, queries, keys, values, out_weight, span_order, document):
    local_heads = queries.shape[1] // HEAD_DIM
    kv_heads = max(1, local_heads // QUERY_GROUP)

    def first_of(group):
        return group * local_heads // QUERY_GROUP

    spans = queries.shape[0] * span_order.shape[0] // document.shape[0]
    if n_grp == 4 and n_ctx == 4 * CORES and kv_heads == 2 and spans == 2:
        return fused(
            queries, keys, values, out_weight, span_order, document, n_ctx, kv_heads, first_of
        )
    attended = gather_attend(
        queries, keys, values, span_order, document, n_ctx, kv_heads, first_of
    )
    partial_value = jnp.dot(attended, out_weight, preferred_element_type=jnp.float32)
    return lax.psum_scatter(
        partial_value.astype(jnp.bfloat16), "grp", scatter_dimension=1, tiled=True
    )


def solution(mesh):
    in_specs = (P("ctx", "grp"), P("ctx", None), P("ctx", None), P("grp", None), P(), P())
    body = functools.partial(shards, mesh.shape["ctx"], mesh.shape["grp"])
    return jax.shard_map(
        body, mesh=mesh, in_specs=in_specs, out_specs=P("ctx", "grp"), check_vma=False
    )
```

time: 63.4 us -> 61.4 us (0.968)
  Pallas kernels: 62.2 us -> 60.3 us
    pallas_call x1, Pallas kernels: 62.2 us -> 60.3 us  [fused(): pl.pallas_call(functools.partial(fused_kernel, n_ctx, kv_heads, first_of)...]
where the time goes in v4:
time: 61.4 us; the launch traced here: 61.3 us
  Pallas kernels  60.3 us (98%)
  local copies, waits for them, and re-layouts  0.97 us (2%)
    pallas_call x1, Pallas kernels, fused(): pl.pallas_call(functools.partial(fused_kernel, n_ctx, kv_heads, first_of)...  60.3 us

profile of v4, /device:TPU:0, one launch (start us, length us, event | category | flops | bytes accessed | tf_op | source)
XLA Modules:
  0.0 61.3 jit_solution(18270273272397784929)
XLA Ops:
  0.0 60.3 %attend_project.1 = bf16[256,2048]{1,0:T(8,128)(2,1)S(1)} custom-call(s32[16]{0:T(128)} %order_hbm.1, s32[16,1,128]{2,1,0:T(1,128)} %bitcast.1, bf16[256,2048]{1,0:T(8,128)(2,1)} %q_hbm.1, bf16[256,1024]{1,0:T(8,128)(2,1)} %k_hbm.1, bf16[256,1024]{1,0:T(8,128)(2,1)} %v_hbm.1, bf16[2048,8192]{1,0:T(8,128)(2,1)} %w_hbm.1), custom_call_target="tpu_custom_call" | custom-call | tf_op jit(solution)/shard_map/attend_project/pallas_call | solution.py:593
  60.3 1.0 %copy.8 = bf16[256,2048]{1,0:T(8,128)(2,1)} copy(bf16[256,2048]{1,0:T(8,128)(2,1)S(1)} %attend_project.1) | data formatting | bytes 2097152

commit v5 on v4

--- a/solution.py
+++ b/solution.py
@@ -145,7 +145,9 @@
         acc_ref[...] = jnp.zeros(acc_ref.shape, jnp.float32)
         order_load.wait()
         doc_load.wait()
-        turned_ref[:, HEAD_DIM:] = jnp.ones((kv_heads, ONES, keys_per_step), turned_ref.dtype)
+        turned_ref[:, HEAD_DIM:] = jnp.ones(
+            (turned_ref.shape[0], ONES, keys_per_step), turned_ref.dtype
+        )
         for at in range(doc_rows.shape[0]):
             doc_cols[at] = jnp.transpose(jnp.broadcast_to(doc_rows[at], (span, span)))
         if more_q is not None:
@@ -212,13 +214,19 @@
                 )
                 more_bias[slot * span : (slot + 1) * span] = jnp.where(seen, 0.0, HIDDEN)
 
-    def turn(block, blocks, h):
+    def keys_at(block, blocks):
+        if blocks == CORES:
+            return slice(None)
+        return pl.ds(pl.multiple_of(block % CORES * tok_rows, tok_rows), blocks * tok_rows)
+
+    def turn(block, blocks, h, spare=0):
         both = kv_all[pl.ds(block, blocks), h].reshape(blocks * tok_rows, 2 * HEAD_DIM)
-        turned_ref[h, :HEAD_DIM] = jnp.transpose(both[:, HEAD_DIM:])
-
-    def attend(chip, h, low, count, own=True, lent=False):
+        turned_ref[h + spare, :HEAD_DIM, keys_at(block, blocks)] = jnp.transpose(both[:, HEAD_DIM:])
+
+    def attend(block, blocks, h, low, count, own=True, lent=False, spare=0):
         rows = pl.ds(low, count)
-        key = kv_all[pl.ds(chip * CORES, CORES), h].reshape(keys_per_step, 2 * HEAD_DIM)
+        keys = keys_at(block, blocks)
+        key = kv_all[pl.ds(block, blocks), h].reshape(blocks * tok_rows, 2 * HEAD_DIM)
         key = key[:, :HEAD_DIM]
         asked = []
         if own:
@@ -235,7 +243,7 @@
             lax.dot_general(
                 key, query, (((1,), (1,)), ((), ())), preferred_element_type=jnp.float32
             )
-            + bias[:, at]
+            + bias[keys, at]
             for query, bias, _, _, at in asked
         ]
         for (_, _, maxes, sums, at), score in zip(asked, scores):
@@ -243,36 +251,48 @@
             top = jnp.maximum(old, jnp.max(score, axis=0, keepdims=True))
             rescale = jnp.exp2((old - top) * factor)
             probs = jnp.exp2((score - top) * factor).astype(jnp.bfloat16)
-            mixed = jnp.dot(turned_ref[h], probs, preferred_element_type=jnp.float32)
+            mixed = jnp.dot(
+                turned_ref[h + spare, :, keys], probs, preferred_element_type=jnp.float32
+            )
             maxes[:, at] = top
             sums[:, at] = sums[:, at] * rescale + mixed
 
     def plan(k):
         middle = near == 1
         after = k - 2
-        first_n = jnp.where(
-            middle, 2 * (after >= 2), (after > 0) * (k + 1) // 2
-        )
-        first_h = jnp.where(middle, after == 3, (after > 0) * (k + 1) % 2)
-        second_n = jnp.where(after == 0, 1, 0)
+        first_n = jnp.where(middle, 2 * (after >= 2), 1 * (after == 0))
+        first_h = jnp.where(middle, 1 * (after == 3), 1)
+        second_n = jnp.where(middle, 1 * (after == 0), (after > 0) * (k + 1) // 2)
+        second_h = jnp.where(middle, 1, (k + 1) % 2)
         chip = jnp.where(
             middle & (after >= 0), chip_of(1 + after % 2), chip_of(k // kv_heads)
         )
         held = jnp.where(middle & (after >= 0), after // 2, k % kv_heads)
-        return first_n, first_h.astype(jnp.int32), second_n, chip, held
+        return first_n, first_h, second_n, second_h, chip, held
+
+    def catch_up():
+        lend().wait_recv()
+        attend(chip_of(1) * CORES, CORES, 0, 0, 0, own=False, lent=True)
+        look(z)
+        for h in range(kv_heads):
+            attend(z * CORES, CORES, h, 0, 0, own=False, lent=True, spare=kv_heads)
 
     def slots(begin, stop, lent):
         def one(k, carry):
-            first_n, first_h, second_n, chip, held = plan(k)
+            first_n, first_h, second_n, second_h, chip, held = plan(k)
             with jax.named_scope("pass_on"):
+                if not lent:
+                    pass_on(1 * (k == 2), 0)
                 pass_on(first_n, first_h)
-                pass_on(second_n, 1)
             look(chip)
             with jax.named_scope("arrive"):
                 arrived(held, chip, 1 - core)
-            turn(chip * CORES, CORES, held)
+            spare = 0 if lent else jnp.where(k < 2, kv_heads, 0)
+            turn(chip * CORES, CORES, held, spare)
             with jax.named_scope("attend"):
-                attend(chip, held, 0, tok_rows, lent=lent)
+                attend(chip * CORES, CORES, held, 0, tok_rows, lent=lent, spare=spare)
+            with jax.named_scope("pass_on"):
+                pass_on(second_n, second_h)
             return carry
 
         lax.fori_loop(begin, stop, one, 0)
@@ -284,7 +304,7 @@
             look(chip_of(n))
             arrived(h, chip_of(n), 1 - core)
             turn(chip_of(n) * CORES, CORES, h)
-            attend(chip_of(n), h, 0, tok_rows)
+            attend(chip_of(n) * CORES, CORES, h, 0, tok_rows)
             return carry
 
         lax.fori_loop(0, nz * kv_heads, one, 0)
@@ -316,7 +336,7 @@
         pltpu.VMEM((slots, 1, span), jnp.int32),
         pltpu.VMEM((rows, heads * HEAD_DIM), bf16),
         pltpu.VMEM((n_ctx, kv_heads, rows, 2 * HEAD_DIM), bf16),
-        pltpu.VMEM((kv_heads, HEAD_DIM + ONES, CORES * rows), bf16),
+        pltpu.VMEM((2 * kv_heads, HEAD_DIM + ONES, CORES * rows), bf16),
         pltpu.VMEM((slots, span, span), jnp.int32),
         pltpu.VMEM((CORES * rows, rows), f32),
         pltpu.VMEM((heads, 1, rows), f32),
@@ -432,8 +452,12 @@
             device_id_type=MESH,
         )
 
+    def swapped(i):
+        return jnp.where(part.core == 1, i + 1 - 2 * (i % 2), i)
+
     def first_far(r):
-        def one(i, carry):
+        def one(at, carry):
+            i = swapped(at)
             send_ref[r, i, : held_rows(r)] = product(r, i).astype(send_ref.dtype)
             send(r, i, i % 2, far_sem.at[r, i])
             return carry
@@ -441,7 +465,8 @@
         lax.fori_loop(0, 4, one, 0)
 
     def first_near(r):
-        def one(i, carry):
+        def one(at, carry):
+            i = swapped(at)
             send_ref[r, i, : held_rows(r)] = product(r, i).astype(send_ref.dtype)
             send(r, i, i % 2, near_sem.at[r])
             return carry
@@ -449,7 +474,8 @@
         lax.fori_loop(4, 8, one, 0)
 
     def second(r):
-        def one(i, carry):
+        def one(at, carry):
+            i = swapped(at)
             value = product(r, i)
             got(r, i - 8, 1, far_sem.at[r, i - 8])
             count = held_rows(r)
@@ -511,24 +537,38 @@
         fetch(i, block_of(i), path_sub(i)[1]).start()
     with jax.named_scope("prepare"):
         part.prepare()
-    part.slots(0, 2, False)
-    with jax.named_scope("pass_on"):
-        part.pass_on(1, 0)
+    part.slots(0, 3, False)
     with jax.named_scope("lent"):
-        pl.when(middle)(lambda: part.lend().wait_recv())
-        for h in range(kv_heads):
-            part.attend(part.z, h, 0, 0, own=False, lent=True)
-    part.slots(2, 6, True)
+        pl.when(middle)(part.catch_up)
+    part.slots(3, 6, True)
     chip = part.chip_of(3)
-    with jax.named_scope("pass_on"):
-        part.pass_on(jnp.where(middle, 0, 3), 1)
     part.look(chip)
-    for h in range(kv_heads):
+    block, own, partners = (
+        chip * CORES, chip * CORES + part.core, chip * CORES + 1 - part.core
+    )
+
+    def whole(h):
+        part.arrived(h, chip, 1 - part.core)
+        part.turn(block, CORES, h)
+        part.attend(block, CORES, h, 0, span, lent=True)
+
+    def halves(h):
+        if h:
+            with jax.named_scope("pass_on"):
+                part.pass_on(3, h)
+        with jax.named_scope("own_half"):
+            part.turn(own, 1, h)
+            part.attend(own, 1, h, 0, span)
         with jax.named_scope("arrive"):
             part.arrived(h, chip, 1 - part.core)
+        with jax.named_scope("other_half"):
+            part.turn(partners, 1, h)
+            part.attend(partners, 1, h, 0, span)
+
+    for h in range(kv_heads):
         with jax.named_scope("attend_0"):
-            part.turn(chip * CORES, CORES, h)
-            part.attend(chip, h, 0, span, lent=True)
+            pl.when(middle)(functools.partial(whole, h))
+            pl.when(jnp.logical_not(middle))(functools.partial(halves, h))
         with jax.named_scope("norm"):
             normalise(0, h)
     with jax.named_scope("first_0"):
@@ -537,7 +577,7 @@
         first_near(0)
     with jax.named_scope("attend_1"):
         for h in range(kv_heads):
-            part.attend(chip, h, span, span)
+            part.attend(block, CORES, h, span, span)
             normalise(1, h)
     with jax.named_scope("first_1_far"):
         first_far(1)

time: 61.4 us -> 60.9 us (level)
  no operation moved by 1% of the time
where the time goes in v5:
time: 60.9 us; the launch traced here: 60.8 us
  Pallas kernels  59.8 us (98%)
  local copies, waits for them, and re-layouts  0.97 us (2%)
    pallas_call x1, Pallas kernels, fused(): pl.pallas_call(functools.partial(fused_kernel, n_ctx, kv_heads, first_of)...  59.8 us

profile of v5, /device:TPU:0, one launch (start us, length us, event | category | flops | bytes accessed | tf_op | source)
XLA Modules:
  0.0 60.8 jit_solution(2652839989247481599)
XLA Ops:
  0.0 59.8 %attend_project.1 = bf16[256,2048]{1,0:T(8,128)(2,1)S(1)} custom-call(s32[16]{0:T(128)} %order_hbm.1, s32[16,1,128]{2,1,0:T(1,128)} %bitcast.1, bf16[256,2048]{1,0:T(8,128)(2,1)} %q_hbm.1, bf16[256,1024]{1,0:T(8,128)(2,1)} %k_hbm.1, bf16[256,1024]{1,0:T(8,128)(2,1)} %v_hbm.1, bf16[2048,8192]{1,0:T(8,128)(2,1)} %w_hbm.1), custom_call_target="tpu_custom_call" | custom-call | tf_op jit(solution)/shard_map/attend_project/pallas_call | solution.py:633
  59.8 1.0 %copy.8 = bf16[256,2048]{1,0:T(8,128)(2,1)} copy(bf16[256,2048]{1,0:T(8,128)(2,1)S(1)} %attend_project.1) | data formatting | bytes 2097152

commit v6 on v5

--- a/solution.py
+++ b/solution.py
@@ -277,7 +277,7 @@
         for h in range(kv_heads):
             attend(z * CORES, CORES, h, 0, 0, own=False, lent=True, spare=kv_heads)
 
-    def slots(begin, stop, lent):
+    def slots(begin, stop, lent, count=None):
         def one(k, carry):
             first_n, first_h, second_n, second_h, chip, held = plan(k)
             with jax.named_scope("pass_on"):
@@ -290,7 +290,9 @@
             spare = 0 if lent else jnp.where(k < 2, kv_heads, 0)
             turn(chip * CORES, CORES, held, spare)
             with jax.named_scope("attend"):
-                attend(chip * CORES, CORES, held, 0, tok_rows, lent=lent, spare=spare)
+                attend(
+                    chip * CORES, CORES, held, 0, count or tok_rows, lent=lent, spare=spare
+                )
             with jax.named_scope("pass_on"):
                 pass_on(second_n, second_h)
             return carry
@@ -455,14 +457,37 @@
     def swapped(i):
         return jnp.where(part.core == 1, i + 1 - 2 * (i % 2), i)
 
-    def first_far(r):
+    half = att_ref.shape[2] // 2
+
+    def early_products():
+        def one(i, carry):
+            own_ref[1, i] = jnp.dot(
+                att_ref[0, :, :half], w_buf[i, :half], preferred_element_type=jnp.float32
+            )
+            return carry
+
+        lax.fori_loop(0, 2, one, 0)
+
+    def late_products():
+        def one(at, carry):
+            i = swapped(at)
+            rest = jnp.dot(
+                att_ref[0, :, half:], w_buf[i, half:], preferred_element_type=jnp.float32
+            )
+            send_ref[0, i] = (own_ref[1, i] + rest).astype(send_ref.dtype)
+            send(0, i, i % 2, far_sem.at[0, i])
+            return carry
+
+        lax.fori_loop(0, 2, one, 0)
+
+    def first_far(r, low=0, high=4):
         def one(at, carry):
             i = swapped(at)
             send_ref[r, i, : held_rows(r)] = product(r, i).astype(send_ref.dtype)
             send(r, i, i % 2, far_sem.at[r, i])
             return carry
 
-        lax.fori_loop(0, 4, one, 0)
+        lax.fori_loop(low, high, one, 0)
 
     def first_near(r):
         def one(at, carry):
@@ -540,7 +565,9 @@
     part.slots(0, 3, False)
     with jax.named_scope("lent"):
         pl.when(middle)(part.catch_up)
-    part.slots(3, 6, True)
+    part.slots(3, 4, True)
+    part.slots(4, 6, True, span)
+    fetched(0)
     chip = part.chip_of(3)
     part.look(chip)
     block, own, partners = (
@@ -559,6 +586,9 @@
         with jax.named_scope("own_half"):
             part.turn(own, 1, h)
             part.attend(own, 1, h, 0, span)
+        if h == kv_heads - 1:
+            with jax.named_scope("early"):
+                early_products()
         with jax.named_scope("arrive"):
             part.arrived(h, chip, 1 - part.core)
         with jax.named_scope("other_half"):
@@ -572,12 +602,23 @@
         with jax.named_scope("norm"):
             normalise(0, h)
     with jax.named_scope("first_0"):
-        fetched(0)
-        first_far(0)
+        pl.when(middle)(lambda: first_far(0, 0, 2))
+        pl.when(jnp.logical_not(middle))(late_products)
+        first_far(0, 2, 4)
         first_near(0)
     with jax.named_scope("attend_1"):
         for h in range(kv_heads):
             part.attend(block, CORES, h, span, span)
+
+        def put_off(k, carry):
+            before, held = part.plan(k)[4:]
+            part.look(before)
+            part.turn(before * CORES, CORES, held)
+            part.attend(before * CORES, CORES, held, span, span)
+            return carry
+
+        lax.fori_loop(4, 6, put_off, 0)
+        for h in range(kv_heads):
             normalise(1, h)
     with jax.named_scope("first_1_far"):
         first_far(1)

time: 60.9 us -> 60.9 us (level)
  no operation moved by 1% of the time
where the time goes in v6:
time: 60.9 us; the launch traced here: 60.7 us
  Pallas kernels  59.8 us (98%)
  local copies, waits for them, and re-layouts  0.97 us (2%)
    pallas_call x1, Pallas kernels, fused(): pl.pallas_call(functools.partial(fused_kernel, n_ctx, kv_heads, first_of)...  59.8 us

profile of v6, /device:TPU:0, one launch (start us, length us, event | category | flops | bytes accessed | tf_op | source)
XLA Modules:
  0.0 60.7 jit_solution(3462012188961511152)
XLA Ops:
  0.0 59.8 %attend_project.1 = bf16[256,2048]{1,0:T(8,128)(2,1)S(1)} custom-call(s32[16]{0:T(128)} %order_hbm.1, s32[16,1,128]{2,1,0:T(1,128)} %bitcast.1, bf16[256,2048]{1,0:T(8,128)(2,1)} %q_hbm.1, bf16[256,1024]{1,0:T(8,128)(2,1)} %k_hbm.1, bf16[256,1024]{1,0:T(8,128)(2,1)} %v_hbm.1, bf16[2048,8192]{1,0:T(8,128)(2,1)} %w_hbm.1), custom_call_target="tpu_custom_call" | custom-call | tf_op jit(solution)/shard_map/attend_project/pallas_call | solution.py:674
  59.8 1.0 %copy.8 = bf16[256,2048]{1,0:T(8,128)(2,1)} copy(bf16[256,2048]{1,0:T(8,128)(2,1)S(1)} %attend_project.1) | data formatting | bytes 2097152
